TPU v7x, 32 devices: a whole 2x2x4 slice. The times are simulated.
32 devices in a mesh: dp: 2 (over x), sp: 16 (over z, y, core).
Axes of the slice: x: 2, y: 2, z: 4, core: 2. Of those that a mesh axis runs over, the one named last changes fastest.
Arguments:
- hidden: bfloat16 [128, 2816], P('dp'), parts along dimension 0
- ln_gamma: float32 [2816], replicated
- ln_beta: float32 [2816], replicated
- w_qkv: bfloat16 [2816, 3072], replicated
- w_out: bfloat16 [2816, 2816], replicated
- w_up: bfloat16 [2816, 11264], P(None, 'sp')
- w_down: bfloat16 [11264, 2816], P('sp')
- k_cache: bfloat16 [128, 8192, 128], P('dp', 'sp'), parts along dimension 0
- v_cache: bfloat16 [128, 8192, 128], P('dp', 'sp'), parts along dimension 0
- positions: int32 [128], P('dp'), parts along dimension 0
Outputs:
- output 1: bfloat16 [128, 2816], P('dp'), parts along dimension 0
- output 2: bfloat16 [128, 8192, 128], P('dp', 'sp'), parts along dimension 0
- output 3: bfloat16 [128, 8192, 128], P('dp', 'sp'), parts along dimension 0
There are 2 independent parts. A program takes and returns all parts, laid end to end along the dimension named above; an argument that names none is the same for every part.
All inputs are finite; a program needn't handle non-finite values.
Results may differ from a plain program's by a relative error of at most 0.00633762.
Values sent between devices are 32-bit elements.
A program may use at most 1 GiB of HBM per device.

v0:
```python
import jax
import jax.numpy as jnp
from jax import lax
from jax.sharding import PartitionSpec as P

LN_EPS = 1e-5
ROPE_BASE = 10000.0
NEG_FILL = -1e30


def layer_norm(hidden, ln_gamma, ln_beta):
    hidden_f32 = hidden.astype(jnp.float32)
    row_mean = jnp.mean(hidden_f32, axis=-1, keepdims=True)
    centered = hidden_f32 - row_mean
    row_var = jnp.mean(centered * centered, axis=-1, keepdims=True)
    return (centered * lax.rsqrt(row_var + LN_EPS) * ln_gamma + ln_beta).astype(jnp.bfloat16)


def rotary_tables(positions, head_dim):
    inv_freq = 1.0 / (ROPE_BASE ** (jnp.arange(0, head_dim, 2, dtype=jnp.float32) / head_dim))
    angles = positions.astype(jnp.float32)[:, None] * inv_freq[None, :]
    cos_half = jnp.cos(angles)
    sin_half = jnp.sin(angles)
    return jnp.concatenate([cos_half, cos_half], axis=-1), jnp.concatenate([sin_half, sin_half], axis=-1)


def apply_rotary(vecs, cos_full, sin_full):
    vecs_f32 = vecs.astype(jnp.float32)
    half_dim = vecs.shape[-1] // 2
    rotated = jnp.concatenate([-vecs_f32[..., half_dim:], vecs_f32[..., :half_dim]], axis=-1)
    return (vecs_f32 * cos_full + rotated * sin_full).astype(jnp.bfloat16)


def local_stats(q_rot, k_block, v_block, local_pos):
    head_dim = q_rot.shape[-1]
    slot_ids = jnp.arange(k_block.shape[1])
    scores = jnp.einsum('bhd,bsd->bhs', q_rot, k_block, preferred_element_type=jnp.float32) * head_dim ** -0.5
    valid_mask = (slot_ids[None, :] <= local_pos[:, None])[:, None, :]
    masked = jnp.where(valid_mask, scores, NEG_FILL)
    block_max = jnp.max(masked, axis=-1)
    exp_scores = jnp.where(valid_mask, jnp.exp(masked - block_max[..., None]), 0.0)
    block_sum = jnp.sum(exp_scores, axis=-1)
    block_ctx = jnp.einsum('bhs,bsd->bhd', exp_scores.astype(jnp.bfloat16), v_block, preferred_element_type=jnp.float32)
    return jnp.concatenate([block_ctx, block_max[..., None], block_sum[..., None]], axis=-1)


def combine_stats(all_stats):
    head_dim = all_stats.shape[-1] - 2
    block_max = all_stats[..., head_dim]
    top_max = jnp.max(block_max, axis=0)
    scale_w = jnp.exp(block_max - top_max[None])
    total_sum = jnp.sum(all_stats[..., head_dim + 1] * scale_w, axis=0)
    total_ctx = jnp.sum(all_stats[..., :head_dim] * scale_w[..., None], axis=0)
    return (total_ctx / total_sum[..., None]).astype(jnp.bfloat16)


def device_step(hidden, ln_gamma, ln_beta, w_qkv, w_out, w_up, w_down, k_cache, v_cache, positions):
    batch_rows = hidden.shape[0]
    seq_dev, head_dim = k_cache.shape[1], k_cache.shape[2]
    num_heads = w_out.shape[0] // head_dim
    normed = layer_norm(hidden, ln_gamma, ln_beta)
    qkv_proj = jnp.dot(normed, w_qkv, preferred_element_type=jnp.float32).astype(jnp.bfloat16)
    qkv_proj = qkv_proj.reshape(batch_rows, num_heads + 2, head_dim)
    cos_full, sin_full = rotary_tables(positions, head_dim)
    q_rot = apply_rotary(qkv_proj[:, :num_heads], cos_full[:, None, :], sin_full[:, None, :])
    k_rot = apply_rotary(qkv_proj[:, num_heads], cos_full, sin_full)
    v_new = qkv_proj[:, num_heads + 1]
    local_pos = positions - lax.axis_index('sp') * seq_dev
    write_mask = (jnp.arange(seq_dev)[None, :] == local_pos[:, None])[:, :, None]
    k_next = jnp.where(write_mask, k_rot[:, None, :], k_cache)
    v_next = jnp.where(write_mask, v_new[:, None, :], v_cache)
    block_stats = local_stats(q_rot, k_next, v_next, local_pos)
    all_stats = lax.all_gather(block_stats, 'sp')
    context = combine_stats(all_stats).reshape(batch_rows, num_heads * head_dim)
    attn_out = jnp.dot(context, w_out, preferred_element_type=jnp.float32)
    up_proj = jnp.dot(normed, w_up, preferred_element_type=jnp.float32)
    activated = jax.nn.gelu(up_proj, approximate=False).astype(jnp.bfloat16)
    mlp_part = jnp.dot(activated, w_down, preferred_element_type=jnp.float32)
    mlp_out = lax.psum(mlp_part, 'sp')
    out_hidden = (hidden.astype(jnp.float32) + attn_out + mlp_out).astype(jnp.bfloat16)
    return out_hidden, k_next, v_next


def solution(mesh):
    cache_spec = P('dp', 'sp', None)
    in_specs = (P('dp', None), P(None), P(None), P(None, None), P(None, None), P(None, 'sp'), P('sp', None), cache_spec, cache_spec, P('dp'))
    out_specs = (P('dp', None), cache_spec, cache_spec)
    return jax.shard_map(device_step, mesh=mesh, in_specs=in_specs, out_specs=out_specs, check_vma=False)
```

profile of v0, /device:TPU:0, one launch (start us, length us, event | category | flops | bytes accessed | tf_op | source)
XLA Modules:
  0.0 275.5 jit_solution(13565472802997640811)
XLA Ops:
  7.2 0.7 fusion.118
  8.4 1.1 convert_reduce_fusion
  9.5 1.3 fusion.17
  10.8 9.4 %fusion.12 = bf16[8,8,24,128]{3,1,2,0:T(8,128)(2,1)S(1)} fusion(bf16[2816,3072]{1,0:T(8,128)(2,1)} %param.13, bf16[64,2816]{1,0:T(8,128)(2,1)} %param.10, f32[2816]{0:T(1024)} %param.12, f32[2816]{0:T(1024)} %param.11, f32[64]{0:T(128)S(1)} %add_rsqrt_fusion, f32[64]{0:T(128)S(1)} %broadcast_multiply_fusion), kind=kOutput, calls=%fused_computation.20 | convolution fusion | flops 1108574208 | bytes 18078208 | tf_op jit(solution)/shard_map/dot_general | solution.py:62
  20.6 1.4 slice_negate_fusion
  22.2 6.8 %broadcast_select_fusion = (bf16[64,512,128]{2,1,0:T(8,128)(2,1)S(1)}, bf16[64,512,128]{2,1,0:T(8,128)(2,1)S(1)}) fusion(bf16[64,512,128]{2,1,0:T(8,128)(2,1)S(1)} %bitcast.42, pred[64,512]{1,0:T(8,128)(4,1)S(1)} %get-tuple-element.18, bf16[64,128]{1,0:T(8,128)(2,1)S(1)} %bitcast.51, bf16[64,512,128]{2,1,0:T(8,128)(2,1)} %param.17, bf16[64,128]{1,0:T(8,128)(2,1)S(1)} %fusion.73), kind=kLoop, calls=%fused_computation.1 | loop fusion | flops 8388608 | bytes 33619968 | tf_op jit(solution)/shard_map/jit(_where)/select_n | solution.py:71
  29.1 7.2 %fusion.2 = (f32[64,22]{1,0:T(8,128)S(1)}, f32[64,22,512]{2,1,0:T(8,128)S(1)}) fusion(pred[64,512]{1,0:T(8,128)(4,1)S(1)} %get-tuple-element.17, bf16[64,512,128]{2,1,0:T(8,128)(2,1)S(1)} %get-tuple-element.11, f32[64,22,64]{2,1,0:T(8,128)} %get-tuple-element.7, f32[64,22,64]{2,1,0:T(8,128)} %get-tuple-element.6, f32[64,128]{1,0:T(8,128)S(1)} %get-tuple-element.24, ...), kind=kOutput, calls=%fused_computation.9 | convolution fusion | flops 187792000 | bytes 12490240 | tf_op jit(solution)/shard_map/bhd,bsd->bhs/dot_general | solution.py:37
  36.2 1.3 fusion.3
  37.5 1.7 fusion.5
  39.2 0.5 copy.46
  39.7 0.5 copy.45
  40.3 0.3 pad_maximum_fusion
  40.5 1.5 copy.47
  42.1 0.2 all-reduce.2.cloned.1.call-start
  42.4 7.0 %fusion.38 = f32[64,2816]{1,0:T(8,128)} fusion(bf16[704,2816]{1,0:T(8,128)(2,1)} %param.16, bf16[2816,704]{0,1:T(8,128)(2,1)} %param.15, bf16[64,2816]{1,0:T(8,128)(2,1)S(1)} %copy-done.2, f32[2816]{0:T(1024)S(1)} %copy-done.3, f32[2816]{0:T(1024)S(1)} %copy-done.4, f32[64]{0:T(128)S(1)} %add_rsqrt_fusion, f32[64]{0:T(128)S(1)} %broadcast_multiply_fusion), kind=kOutput, calls=%fused_computation.63 | convolution fusion | flops 511520768 | bytes 9034240 | tf_op jit(solution)/shard_map/dot_general | solution.py:78
  49.4 114.2 %all-gather.3.cloned.1.call-done = f32[1024,22,130]{2,0,1:T(8,128)} async-done(((f32[64,22,130]{2,0,1:T(8,128)}), f32[1024,22,130]{2,0,1:T(8,128)}) %all-gather.3.cloned.1.call-update) | async-done | bytes 11714576 | tf_op jit(solution)/shard_map/all_gather | solution.py:73
  163.6 16.0 %fusion.116 = (f32[16,64,22,1]{3,1,0,2:T(8,128)}, f32[64,22]{0,1:T(8,128)S(1)}, f32[16,64,22,1]{3,1,0,2:T(8,128)}) fusion(f32[16,64,22,130]{3,1,0,2:T(8,128)} %bitcast.39), kind=kLoop, calls=%fused_computation.150 | loop fusion | flops 21120 | bytes 366080 | tf_op jit(solution)/shard_map/slice | solution.py:52
  179.6 10.9 %slice.47 = f32[16,64,22,128]{3,1,0,2:T(8,128)} slice(f32[16,64,22,130]{3,1,0,2:T(8,128)} %bitcast.40), slice={[0:16], [0:64], [0:22], [0:128]} | slice | bytes 23068672 | tf_op jit(solution)/shard_map/slice | solution.py:53
  190.5 6.6 %copy.58 = f32[16,64,22,1]{1,0,3,2:T(8,128)S(1)} copy(f32[16,64,22,1]{3,1,0,2:T(8,128)} %get-tuple-element.5) | data formatting | bytes 180224
  197.2 6.6 %copy.59 = f32[16,64,22,1]{1,0,3,2:T(8,128)S(1)} copy(f32[16,64,22,1]{3,1,0,2:T(8,128)} %get-tuple-element.3) | data formatting | bytes 180224
  203.8 17.2 %copy.57 = f32[16,64,22,128]{1,0,3,2:T(8,128)} copy(f32[16,64,22,128]{3,1,0,2:T(8,128)} %slice.47) | data formatting | bytes 23068672
  221.0 13.9 %multiply_reduce_fusion = f32[64,22,128]{0,2,1:T(8,128)S(1)} fusion(f32[16,64,22,128]{1,0,3,2:T(8,128)} %copy.57, f32[16,64,22]{1,0,2:T(8,128)S(1)} %exponential_bitcast_fusion), kind=kLoop, calls=%fused_computation | loop fusion | flops 5586944 | bytes 12345344 | tf_op jit(solution)/shard_map/reduce_sum | solution.py:53
  235.2 24.2 %all-reduce.2.cloned.1.call-done = f32[64,2816]{1,0:T(8,128)} async-done(((f32[64,2816]{1,0:T(8,128)}), f32[64,2816]{1,0:T(8,128)}) %all-reduce.2.cloned.1.call-update) | async-done | bytes 720912 | tf_op jit(solution)/shard_map/psum | solution.py:79
  259.4 9.3 %fusion.1 = bf16[64,2816]{1,0:T(8,128)(2,1)} fusion(f32[64,2816]{1,0:T(8,128)} %all-reduce.2.cloned.1.call-done, bf16[64,2816]{0,1:T(8,128)(2,1)S(1)} %bitcast.43, bf16[2816,2816]{1,0:T(8,128)(2,1)} %param.14, bf16[64,2816]{1,0:T(8,128)(2,1)S(1)} %copy-done.2), kind=kOutput, calls=%fused_computation.5 | convolution fusion | flops 1015742464 | bytes 17661952 | tf_op jit(solution)/shard_map/dot_general | solution.py:75
  (34 shorter events, 1.3 us)
Async XLA Ops:
  7.2 156.4 %all-gather.3.cloned.1.call-start = ((), (), s32[]{:S(2)}) async-start(), calls=%async_computation.1 | async-start | bytes 24510464 | tf_op jit(solution)/shard_map/all_gather | solution.py:73
  10.8 11.4 %slice-start = ((s8[8388608]{0:T(1024)(128)(4,1)}), s8[4194304]{0:T(1024)(128)(4,1)S(1)}, s32[]{:S(2)}) async-start(s8[8388608]{0:T(1024)(128)(4,1)} %bitcast.41), calls=%async_computation.2 | async-start | bytes 8388608
  10.8 11.4 %slice-start.1 = ((s8[8388608]{0:T(1024)(128)(4,1)}), s8[4194304]{0:T(1024)(128)(4,1)S(1)}, s32[]{:S(2)}) async-start(s8[8388608]{0:T(1024)(128)(4,1)} %bitcast.41), calls=%async_computation.3 | async-start | bytes 8388608
  29.0 8.5 %copy-start = (bf16[64,512,128]{2,1,0:T(8,128)(2,1)}, bf16[64,512,128]{2,1,0:T(8,128)(2,1)S(1)}, u32[]{:S(2)}) copy-start(bf16[64,512,128]{2,1,0:T(8,128)(2,1)S(1)} %get-tuple-element.10) | copy-start | bytes 25165828
  29.1 10.1 %copy-start.1 = (bf16[64,512,128]{2,1,0:T(8,128)(2,1)}, bf16[64,512,128]{2,1,0:T(8,128)(2,1)S(1)}, u32[]{:S(2)}) copy-start(bf16[64,512,128]{2,1,0:T(8,128)(2,1)S(1)} %get-tuple-element.11) | copy-start | bytes 25165828
  40.2 2.1 copy-start.2
  40.2 2.1 copy-start.3
  40.2 2.1 copy-start.4
  42.1 217.3 %all-reduce.2.cloned.1.call-start = ((), (), s32[]{:S(2)}) async-start(), calls=%async_computation | async-start | bytes 1441792 | tf_op jit(solution)/shard_map/psum | solution.py:79
Sparse Core Ops, SparseCore 0:
  42.2 121.2 all-gather.2
  167.0 92.3 all-reduce.1
where the time goes:
time: 276 us
  waiting for transfers between devices  138 us (50%)
  other arithmetic  44 us (16%)
  local copies, waits for them, and re-layouts  44 us (16%)
  matrix products  34.5 us (12%)
  between operations  14.3 us (5%)
    all_gather x1, waiting for transfers between devices, device_step(): all_stats = lax.all_gather(block_stats, 'sp')  114 us
    unnamed x19, local copies, waits for them, and re-layouts  30.5 us
    psum x1, waiting for transfers between devices, device_step(): mlp_out = lax.psum(mlp_part, 'sp')  24.2 us
    slice x1, other arithmetic, combine_stats(): total_sum = jnp.sum(all_stats[..., head_dim + 1] * scale_w, axis=0)  16 us
    reduce_sum x1, other arithmetic, combine_stats(): total_ctx = jnp.sum(all_stats[..., :head_dim] * scale_w[..., None], axis=0)  13.9 us
    slice x1, local copies, waits for them, and re-layouts, combine_stats(): total_ctx = jnp.sum(all_stats[..., :head_dim] * scale_w[..., None], axis=0)  10.9 us
    dot_general x1, matrix products, device_step(): jnp.dot(normed, w_qkv, preferred_element_type=jnp.float32)  9.4 us
    dot_general x1, matrix products, device_step(): attn_out = jnp.dot(context, w_out, preferred_element_type=jnp.float32)  9.28 us
  transfers between devices with their start and end apart: 2, of which 2 were waited for; matrix products, arithmetic and copies ran while one was open for 29% of the time, Pallas kernels for 0%

commit v1 on v0

v1 whole, which is shorter than its diff:
```python
import functools
import math

import jax
import jax.numpy as jnp
from jax import lax
from jax.experimental import pallas as pl
from jax.experimental.pallas import tpu as pltpu
from jax.sharding import PartitionSpec as P

LN_EPS = 1e-5
ROPE_BASE = 10000.0
NEG_FILL = -1e30
MESH = pl.DeviceIdType.MESH

ROWS = 64
D = 2816
HD = 128
NH = 22
HALF = 11
FF = 704
SEQ = 512
GROUPS = 8
LANE_L = 64
QCHUNK = 512
NQ = 6
QSLOTS = 4
F32 = jnp.float32
BF16 = jnp.bfloat16


def rope(vec, cos, sin_signed):
    return (vec * cos + pltpu.roll(vec, HD // 2, 1) * sin_signed).astype(BF16).astype(F32)


def remote(src, dst, ssem, rsem, dev):
    return pltpu.make_async_remote_copy(src, dst, ssem, rsem, device_id=dev, device_id_type=MESH)


def weights_of(tile, top):
    return jnp.exp(tile - top)


def main_kernel(pos, x_ref, g_ref, b_ref, cos_ref, sin_ref, wqkv, wout, wup, wdn, kh, vh,
                agb, ko, vo,
                wq, wu, wd, h_s, act, q4, kn, vn,
                st, d2d, cmb, rcv, ml, mld, mls, mly, mlz, mlr, wsend, wrecv,
                qsem, osem, ksem, vsem,
                d2d_s, d2d_r, a2a_s, a2a_r, mld_s, mld_r, mly_s, mly_r, mlz_s, mlz_r, wo_s, wo_r,
                agz_s, agz_r, agy_s, agy_r, agc_s, agc_r):
    dp = lax.axis_index("dp")
    me = lax.axis_index("sp")
    core = me % 2
    chip = me // 2
    y = chip % 2
    z = chip // 2
    partner = (dp, me + 1 - 2 * core)
    ypeer = (dp, me + 2 - 4 * y)

    def zpeer(d):
        return (dp, ((z + d) % 4) * 4 + y * 2 + core)

    def cpeer(d):
        return (dp, ((chip + d) % 8) * 2 + core)

    c_q = [pltpu.make_async_copy(wqkv.at[:, pl.ds(QCHUNK * i, QCHUNK)], wq.at[i % QSLOTS], qsem.at[i]) for i in range(NQ)]

    def c_kv(s):
        rows = pl.ds(8 * ((chip + s + 1) % 8), 8)
        return (pltpu.make_async_copy(kh.at[rows], ko.at[rows], ksem.at[s]),
                pltpu.make_async_copy(vh.at[rows], vo.at[rows], vsem.at[s]))

    def start_kv(s):
        for c in c_kv(s):
            c.start()

    c_o = [pltpu.make_async_copy(wout.at[pl.ds((2 * core + i) * FF, FF)], (wu, wd)[i], osem.at[i]) for i in range(2)]

    for i in range(QSLOTS):
        c_q[i].start()

    barrier = pltpu.get_barrier_semaphore()
    pl.semaphore_signal(barrier, inc=1, device_id=partner, device_id_type=MESH)
    for d in range(1, GROUPS):
        pl.semaphore_signal(barrier, inc=1, device_id=cpeer(d), device_id_type=MESH)

    def norm_rows(i, carry):
        rows = pl.ds(pl.multiple_of(16 * i, 16), 16)
        xf = x_ref[rows, :].astype(F32)
        cen = xf - jnp.mean(xf, axis=-1, keepdims=True)
        var = jnp.mean(cen * cen, axis=-1, keepdims=True)
        h_s[rows, :] = (cen * lax.rsqrt(var + LN_EPS) * g_ref[...] + b_ref[...]).astype(BF16)
        return carry

    lax.fori_loop(0, ROWS // 16, norm_rows, 0)

    up = lax.dot_general(h_s[...], wup[...], (((1,), (1,)), ((), ())), preferred_element_type=F32)
    act[...] = (0.5 * up * (1.0 + lax.erf(up * (1.0 / math.sqrt(2.0))))).astype(BF16)
    for n in range(HALF):
        part = jnp.dot(act[...], wdn[:, 256 * n:256 * (n + 1)], preferred_element_type=F32)
        for j in (2 * n, 2 * n + 1):
            ml[:, j // HALF, j % HALF] = part[:, 128 * (j - 2 * n):128 * (j - 2 * n + 1)].reshape(GROUPS, 8, HD)
    pl.semaphore_wait(barrier, GROUPS)
    r_mld = remote(ml.at[:, 1 - core], mld, mld_s, mld_r, partner)
    r_mld.start()

    cos = cos_ref[...]
    sin = sin_ref[...]
    r_mly = remote(mls.at[:, 1 - y], mly, mly_s, mly_r, ypeer)
    for ch in range(NQ):
        c_q[ch].wait()
        acc = jnp.dot(h_s[...], wq[ch % QSLOTS], preferred_element_type=F32).astype(BF16).astype(F32)
        if ch + QSLOTS < NQ:
            c_q[ch + QSLOTS].start()
        if ch >= 2:
            start_kv(ch - 2)
        for i in range(QCHUNK // HD):
            h = ch * (QCHUNK // HD) + i
            vec = acc[:, HD * i:HD * (i + 1)]
            if h <= NH:
                vec = rope(vec, cos, sin)
            vec = vec.reshape(GROUPS, 8, HD)
            if h < NH:
                q4[:, h] = vec
            elif h == NH:
                kn[...] = vec
            else:
                vn[...] = vec
        if ch == 2:
            r_mld.wait_recv()
            mls[...] = ml[:, core].reshape(4, 2, HALF, 8, HD) + mld[...].reshape(4, 2, HALF, 8, HD)
            r_mly.start()

    row_id = lax.broadcasted_iota(jnp.int32, (SEQ, HD), 0)
    col_id = lax.broadcasted_iota(jnp.int32, (NH, SEQ), 1)
    sub = lax.broadcasted_iota(jnp.int32, (NH, HD), 0)
    lane = lax.broadcasted_iota(jnp.int32, (NH, HD), 1)

    def attend(s):
        p = (chip + s + 1) % 8
        for r in range(8):
            b = 8 * p + r
            local = pos[b] - me * SEQ
            here = row_id == local
            kb = jnp.where(here, jnp.broadcast_to(kn[p, r:r + 1, :], (SEQ, HD)).astype(BF16), ko[b])
            vb = jnp.where(here, jnp.broadcast_to(vn[p, r:r + 1, :], (SEQ, HD)).astype(BF16), vo[b])
            ko[b] = kb
            vo[b] = vb
            q = q4[p, :, r, :].astype(BF16)
            sc = lax.dot_general(q, kb, (((1,), (1,)), ((), ())), preferred_element_type=F32) * HD ** -0.5
            valid = col_id <= local
            sc = jnp.where(valid, sc, NEG_FILL)
            m = jnp.max(sc, axis=-1, keepdims=True)
            e = jnp.where(valid, jnp.exp(sc - m), 0.0)
            l = jnp.sum(e, axis=-1, keepdims=True)
            o = jnp.dot(e.astype(BF16), vb, preferred_element_type=F32)
            for half in range(2):
                idx = sub - HALF * half
                own = (idx >= 0) & (idx < HALF)
                t = jnp.where(own & (lane == idx), m, jnp.where(own & (lane == idx + LANE_L), l, 0.0))
                st[s, half, HALF, r:r + 1, :] = jnp.sum(t, axis=0, keepdims=True)
                st[s, half, 0:HALF, r, :] = o[HALF * half:HALF * (half + 1), :]

    def r_d2d(s):
        return remote(st.at[s, 1 - core], d2d.at[s], d2d_s.at[s], d2d_r.at[s], partner)

    def r_a2a(s):
        return remote(cmb.at[s], rcv.at[s], a2a_s.at[s], a2a_r.at[s], cpeer(s + 1))

    lane8 = lax.broadcasted_iota(jnp.int32, (8, HD), 1)

    def pair(s):
        r_d2d(s).wait_recv()
        ta, tb = st[s, core, HALF], d2d[s, HALF]
        top = jnp.maximum(ta, tb)
        wa, wb = weights_of(ta, top), weights_of(tb, top)
        total = ta * pltpu.roll(wa, LANE_L, 1) + tb * pltpu.roll(wb, LANE_L, 1)
        cmb[s, HALF] = jnp.where(lane8 < LANE_L, top, total)
        for i in range(HALF):
            cmb[s, i] = st[s, core, i] * wa[:, i:i + 1] + d2d[s, i] * wb[:, i:i + 1]

    r_mlz = [remote(mlz.at[(z + d) % 4], mlr.at[d - 1], mlz_s.at[d - 1], mlz_r.at[d - 1], zpeer(d)) for d in range(1, 4)]

    def step(s, carry):
        ck, cv = c_kv(s)
        ck.wait()
        cv.wait()

        @pl.when(s < 4)
        def _():
            start_kv(s + 4)

        @pl.when(s == 4)
        def _():
            c_o[0].start()

        @pl.when(s == 5)
        def _():
            c_o[1].start()

        @pl.when(s == 1)
        def _():
            r_mly.wait_recv()
            mlz[...] = mls[:, y] + mly[...]
            for c in r_mlz:
                c.start()

        attend(s)
        r_d2d(s).start()

        @pl.when(s > 0)
        def _():
            pair(s - 1)
            r_a2a(s - 1).start()

        return carry

    lax.fori_loop(0, GROUPS, step, 0)
    pair(GROUPS - 1)

    for c in r_mlz:
        c.wait_recv()
    fin = mlz[z] + mlr[0] + mlr[1] + mlr[2]

    for s in range(GROUPS - 1):
        r_a2a(s).wait_recv()
    tiles = [cmb[GROUPS - 1, HALF]] + [rcv[s, HALF] for s in range(GROUPS - 1)]
    top = functools.reduce(jnp.maximum, tiles)
    ws = [weights_of(t, top) for t in tiles]
    total = functools.reduce(jnp.add, [t * pltpu.roll(w, LANE_L, 1) for t, w in zip(tiles, ws)])
    heads = []
    for i in range(HALF):
        acc = cmb[GROUPS - 1, i] * ws[0][:, i:i + 1]
        for s in range(GROUPS - 1):
            acc += rcv[s, i] * ws[s + 1][:, i:i + 1]
        heads.append((acc / total[:, LANE_L + i:LANE_L + i + 1]).astype(BF16))
    ctx = jnp.concatenate(heads, axis=1)

    def project(column_half):
        cols = pl.ds(pl.multiple_of(HALF * HD * column_half, HD), HALF * HD)
        return (jnp.dot(ctx[:, :FF], wu[:, cols], preferred_element_type=F32)
                + jnp.dot(ctx[:, FF:], wd[:, cols], preferred_element_type=F32))

    c_o[0].wait()
    c_o[1].wait()
    other = project(1 - core)
    for i in range(HALF):
        wsend[i] = other[:, HD * i:HD * (i + 1)]
    r_wo = remote(wsend, wrecv, wo_s, wo_r, partner)
    r_wo.start()
    mine = project(core)
    r_wo.wait_recv()
    for i in range(HALF):
        agb[chip, core, i] = mine[:, HD * i:HD * (i + 1)] + wrecv[i] + fin[i]

    def piece(zz, yy):
        return agb.at[zz * 2 + yy, core]

    def send_z(d):
        return remote(piece(z, y), piece(z, y), agz_s.at[d - 1], agz_r.at[d - 1], zpeer(d))

    def send_y(d):
        zz = (z + 4 - d) % 4
        return remote(piece(zz, y), piece(zz, y), agy_s.at[d], agy_r.at[d], ypeer)

    def send_c(d, other_y):
        zz = (z + 4 - d) % 4
        yy = (y + other_y) % 2
        return remote(piece(zz, yy), piece(zz, yy), agc_s.at[2 * d + other_y], agc_r.at[2 * d + other_y], partner)

    for d in (2, 1, 3):
        send_z(d).start()
    send_y(0).start()
    send_c(0, 0).start()
    for d in (1, 2, 3):
        send_z(d).wait_recv()
        send_y(d).start()
        send_c(d, 0).start()
    for d in range(4):
        send_y(d).wait_recv()
        send_c(d, 1).start()
    for d in range(4):
        for o in range(2):
            send_c(d, o).wait_recv()

    r_mld.wait_send()
    r_mly.wait_send()
    for c in r_mlz:
        c.wait_send()
    for s in range(GROUPS):
        r_d2d(s).wait_send()
    for s in range(GROUPS - 1):
        r_a2a(s).wait_send()
    r_wo.wait_send()
    for d in (1, 2, 3):
        send_z(d).wait_send()
    for d in range(4):
        send_y(d).wait_send()
        send_c(d, 0).wait_send()
        send_c(d, 1).wait_send()


def write_kernel(ko, vo, agb, x_ref, out_ref, k_out, v_out, sem):
    copies = []
    for i in range(8):
        rows = pl.ds(8 * i, 8)
        copies.append(pltpu.make_async_copy(ko.at[rows], k_out.at[rows], sem.at[2 * i]))
        copies.append(pltpu.make_async_copy(vo.at[rows], v_out.at[rows], sem.at[2 * i + 1]))
    for c in copies:
        c.start()
    for q in range(GROUPS // 2):
        rows = slice(16 * q, 16 * (q + 1))
        for j in range(NH):
            cols = slice(HD * j, HD * (j + 1))
            both = agb[2 * q:2 * q + 2, j // HALF, j % HALF].reshape(16, HD)
            out_ref[rows, cols] = (x_ref[rows, cols].astype(F32) + both).astype(BF16)
    for c in copies:
        c.wait()


def device_step(hidden, ln_gamma, ln_beta, w_qkv, w_out, w_up, w_down, k_cache, v_cache, positions):
    inv_freq = 1.0 / (ROPE_BASE ** (jnp.arange(0, HD, 2, dtype=F32) / HD))
    angles = positions.astype(F32)[:, None] * inv_freq[None, :]
    cos, sin = jnp.cos(angles), jnp.sin(angles)
    cos_full = jnp.concatenate([cos, cos], axis=-1)
    sin_signed = jnp.concatenate([-sin, sin], axis=-1)

    vmem = pl.BlockSpec(memory_space=pltpu.VMEM)
    hbm = pl.BlockSpec(memory_space=pltpu.HBM)
    smem = pl.BlockSpec(memory_space=pltpu.SMEM)
    dma = pltpu.SemaphoreType.DMA
    agb, k_new, v_new = pl.pallas_call(
        main_kernel,
        out_shape=(
            jax.ShapeDtypeStruct((GROUPS, 2, HALF, 8, HD), F32),
            jax.ShapeDtypeStruct(k_cache.shape, BF16),
            jax.ShapeDtypeStruct(v_cache.shape, BF16),
        ),
        in_specs=[smem] + [vmem] * 5 + [hbm] * 2 + [vmem] * 2 + [hbm] * 2,
        out_specs=(vmem, vmem, vmem),
        scratch_shapes=[
            pltpu.VMEM((QSLOTS, D, QCHUNK), BF16),
            pltpu.VMEM((FF, D), BF16),
            pltpu.VMEM((FF, D), BF16),
            pltpu.VMEM((ROWS, D), BF16),
            pltpu.VMEM((ROWS, FF), BF16),
            pltpu.VMEM((GROUPS, NH, 8, HD), F32),
            pltpu.VMEM((GROUPS, 8, HD), F32),
            pltpu.VMEM((GROUPS, 8, HD), F32),
            pltpu.VMEM((GROUPS, 2, HALF + 1, 8, HD), F32),
            pltpu.VMEM((GROUPS, HALF + 1, 8, HD), F32),
            pltpu.VMEM((GROUPS, HALF + 1, 8, HD), F32),
            pltpu.VMEM((GROUPS - 1, HALF + 1, 8, HD), F32),
            pltpu.VMEM((GROUPS, 2, HALF, 8, HD), F32),
            pltpu.VMEM((GROUPS, HALF, 8, HD), F32),
            pltpu.VMEM((4, 2, HALF, 8, HD), F32),
            pltpu.VMEM((4, HALF, 8, HD), F32),
            pltpu.VMEM((4, HALF, 8, HD), F32),
            pltpu.VMEM((3, HALF, 8, HD), F32),
            pltpu.VMEM((HALF, 8, HD), F32),
            pltpu.VMEM((HALF, 8, HD), F32),
            dma((NQ,)), dma((2,)), dma((GROUPS,)), dma((GROUPS,)),
            dma((GROUPS,)), dma((GROUPS,)), dma((GROUPS - 1,)), dma((GROUPS - 1,)),
            dma, dma, dma, dma, dma((3,)), dma((3,)), dma, dma,
            dma((3,)), dma((3,)), dma((4,)), dma((4,)), dma((8,)), dma((8,)),
        ],
        compiler_params=pltpu.CompilerParams(collective_id=0, has_side_effects=True, vmem_limit_bytes=28 * 2**20),
        name="layer",
    )(positions, hidden, ln_gamma.reshape(1, D), ln_beta.reshape(1, D), cos_full, sin_signed,
      w_qkv, w_out, w_up.T, w_down, k_cache, v_cache)

    return pl.pallas_call(
        write_kernel,
        out_shape=(
            jax.ShapeDtypeStruct(hidden.shape, BF16),
            jax.ShapeDtypeStruct(k_cache.shape, BF16),
            jax.ShapeDtypeStruct(v_cache.shape, BF16),
        ),
        in_specs=[vmem] * 4,
        out_specs=(vmem, hbm, hbm),
        scratch_shapes=[dma((16,))],
        compiler_params=pltpu.CompilerParams(vmem_limit_bytes=16 * 2**20),
        name="write",
    )(k_new, v_new, agb, hidden)


def solution(mesh):
    cache_spec = P('dp', 'sp', None)
    in_specs = (P('dp', None), P(None), P(None), P(None, None), P(None, None), P(None, 'sp'), P('sp', None), cache_spec, cache_spec, P('dp'))
    out_specs = (P('dp', None), cache_spec, cache_spec)
    return jax.shard_map(device_step, mesh=mesh, in_specs=in_specs, out_specs=out_specs, check_vma=False)
```

time: 276 us -> 64.2 us (0.23)
  waiting for transfers between devices: 138 us -> 0 us
  Pallas kernels: 0 us -> 54.9 us
  other arithmetic: 44 us -> 0.95 us
  local copies, waits for them, and re-layouts: 44 us -> 7.31 us
  matrix products: 34.5 us -> 0 us
  between operations: 14.3 us -> 0.67 us
    all_gather x1 -> x0, waiting for transfers between devices: 114 us -> none  [device_step(): all_stats = lax.all_gather(block_stats, 'sp')]
    pallas_call x0 -> x2, Pallas kernels: none -> 54.9 us  [the longest x1 48.2 us: device_step(): pl.pallas_call(main_kernel, out_shape=(jax.ShapeDtypeStruct((GROUPS, 2, H...]
    dot_general x5 -> x0, matrix products: 34.5 us -> none  [the longest x1 9.4 us: device_step(): jnp.dot(normed, w_qkv, preferred_element_type=jnp.float32)]
    unnamed x19 -> x8, local copies, waits for them, and re-layouts: 30.5 us -> 5.88 us
    psum x1 -> x0, waiting for transfers between devices: 24.2 us -> none  [device_step(): mlp_out = lax.psum(mlp_part, 'sp')]
    reduce_sum x5 -> x0, other arithmetic: 17.7 us -> none  [the longest x1 13.9 us: combine_stats(): total_ctx = jnp.sum(all_stats[..., :head_dim] * scale_w[..., None], axis=0)]
    slice x2 -> x0, other arithmetic: 16.1 us -> none  [the longest x1 16 us: combine_stats(): total_sum = jnp.sum(all_stats[..., head_dim + 1] * scale_w, axis=0)]
    slice x1 -> x0, local copies, waits for them, and re-layouts: 10.9 us -> none  [combine_stats(): total_ctx = jnp.sum(all_stats[..., :head_dim] * scale_w[..., None], axis=0)]
  transfers between devices with their start and end apart: 2 -> 0, of which waited for: 2 -> 0; matrix products, arithmetic and copies ran while one was open for 29% -> 0% of each run, Pallas kernels for 0% -> 0%
where the time goes in v1:
time: 64.2 us; the launch traced here: 63.8 us
  Pallas kernels  54.9 us (86%)
  local copies, waits for them, and re-layouts  7.31 us (11%)
  other arithmetic  0.95 us (1%)
  between operations  0.67 us (1%)
    pallas_call x1, Pallas kernels, device_step(): pl.pallas_call(main_kernel, out_shape=(jax.ShapeDtypeStruct((GROUPS, 2, H...  48.2 us
    pallas_call x1, Pallas kernels, device_step(): pl.pallas_call(write_kernel, out_shape=(jax.ShapeDtypeStruct(hidden.shape...  6.7 us
    unnamed x8, local copies, waits for them, and re-layouts  5.88 us

profile of v1, /device:TPU:0, one launch (start us, length us, event | category | flops | bytes accessed | tf_op | source)
XLA Modules:
  0.0 63.8 jit_solution(10390720407616065069)
XLA Ops:
  0.6 0.7 %convert_element_type.3 = f32[64]{0:T(128)S(1)} convert(s32[64]{0:T(128)} %pos.1) | non-fusion elementwise | flops 64 | bytes 512 | tf_op jit(solution)/shard_map/convert_element_type | solution.py:323
  1.3 0.7 %reshape.19.g_ref = f32[1,2816]{1,0:T(1,128)S(1)} reshape(f32[2816]{0:T(1024)} %param.11) | data formatting | bytes 22528 | tf_op jit(solution)/shard_map/reshape | solution.py:369
  2.0 0.7 %reshape.20.b_ref = f32[1,2816]{1,0:T(1,128)S(1)} reshape(f32[2816]{0:T(1024)} %param.12) | data formatting | bytes 22528 | tf_op jit(solution)/shard_map/reshape | solution.py:369
  2.7 0.2 fusion
  2.9 0.1 pad_maximum_fusion
  3.0 0.0 copy-start
  3.0 2.1 %copy-done = bf16[2816,704]{0,1:T(8,128)(2,1)S(1)} copy-done((bf16[2816,704]{0,1:T(8,128)(2,1)S(1)}, bf16[2816,704]{0,1:T(8,128)(2,1)}, u32[]{:S(2)}) %copy-start) | copy-done | bytes 3964952
  5.2 0.0 copy-start.1
  5.2 2.1 %copy-done.1 = bf16[704,2816]{1,0:T(8,128)(2,1)S(1)} copy-done((bf16[704,2816]{1,0:T(8,128)(2,1)S(1)}, bf16[704,2816]{1,0:T(8,128)(2,1)}, u32[]{:S(2)}) %copy-start.1) | copy-done | bytes 3964952
  7.3 0.0 copy-start.2
  7.3 1.0 %copy-done.2 = bf16[64,2816]{1,0:T(8,128)(2,1)S(1)} copy-done((bf16[64,2816]{1,0:T(8,128)(2,1)S(1)}, bf16[64,2816]{1,0:T(8,128)(2,1)}, u32[]{:S(2)}) %copy-start.2) | copy-done | bytes 360472
  8.3 0.0 copy-start.3
  8.3 0.7 %copy-done.3 = s32[64]{0:T(128)S(1)} copy-done((s32[64]{0:T(128)S(1)}, s32[64]{0:T(128)}, u32[]{:S(2)}) %copy-start.3) | copy-done | bytes 280
  8.9 48.2 %layer.1 = (f32[8,2,11,8,128]{4,3,2,1,0:T(8,128)S(1)}, bf16[64,512,128]{2,1,0:T(8,128)(2,1)S(1)}, bf16[64,512,128]{2,1,0:T(8,128)(2,1)S(1)}) custom-call(s32[64]{0:T(128)S(1)} %copy-done.3, bf16[64,2816]{1,0:T(8,128)(2,1)S(1)} %copy-done.2, f32[1,2816]{1,0:T(1,128)S(1)} %reshape.19.g_ref, f32[1,2816]{1,0:T(1,128)S(1)} %reshape.20.b_ref, ...), custom_call_target="tpu_custom_call" | custom-call | tf_op jit(solution)/shard_map/layer/pallas_call | solution.py:332
  57.1 6.7 %write.1 = (bf16[64,2816]{1,0:T(8,128)(2,1)}, bf16[64,512,128]{2,1,0:T(8,128)(2,1)}, bf16[64,512,128]{2,1,0:T(8,128)(2,1)}) custom-call(bf16[64,512,128]{2,1,0:T(8,128)(2,1)S(1)} %get-tuple-element.6.ko, bf16[64,512,128]{2,1,0:T(8,128)(2,1)S(1)} %get-tuple-element.7.vo, f32[8,2,11,8,128]{4,3,2,1,0:T(8,128)S(1)} %get-tuple-element.8.agb, ...), custom_call_target="tpu_custom_call" | custom-call | tf_op jit(solution)/shard_map/write/pallas_call | solution.py:372
  (1 shorter events, 0.0 us)
Async XLA Ops:
  3.0 2.1 %copy-start = (bf16[2816,704]{0,1:T(8,128)(2,1)S(1)}, bf16[2816,704]{0,1:T(8,128)(2,1)}, u32[]{:S(2)}) copy-start(bf16[2816,704]{0,1:T(8,128)(2,1)} %param.15) | copy-start | bytes 11894788
  5.2 2.1 %copy-start.1 = (bf16[704,2816]{1,0:T(8,128)(2,1)S(1)}, bf16[704,2816]{1,0:T(8,128)(2,1)}, u32[]{:S(2)}) copy-start(bf16[704,2816]{1,0:T(8,128)(2,1)} %wdn.1) | copy-start | bytes 11894788
  7.3 1.0 %copy-start.2 = (bf16[64,2816]{1,0:T(8,128)(2,1)S(1)}, bf16[64,2816]{1,0:T(8,128)(2,1)}, u32[]{:S(2)}) copy-start(bf16[64,2816]{1,0:T(8,128)(2,1)} %x_ref.3) | copy-start | bytes 1081348
  8.3 0.7 %copy-start.3 = (s32[64]{0:T(128)S(1)}, s32[64]{0:T(128)}, u32[]{:S(2)}) copy-start(s32[64]{0:T(128)} %pos.1) | copy-start | bytes 772

commit v2 on v1

--- a/solution.py
+++ b/solution.py
@@ -3,6 +3,7 @@
 
 import jax
 import jax.numpy as jnp
+import numpy as np
 from jax import lax
 from jax.experimental import pallas as pl
 from jax.experimental.pallas import tpu as pltpu
@@ -41,11 +42,11 @@
     return jnp.exp(tile - top)
 
 
-def main_kernel(pos, x_ref, g_ref, b_ref, cos_ref, sin_ref, wqkv, wout, wup, wdn, kh, vh,
-                agb, ko, vo,
-                wq, wu, wd, h_s, act, q4, kn, vn,
+def main_kernel(pos_h, x_h, g_h, b_h, freq_h, wqkv, wout, wup, wdn, kh, vh,
+                agb, ko, vo, kn, vn,
+                pos, x_s, g_s, b_s, freq_s, posv, wq, wu, wd, h_s, act, q4,
                 st, d2d, cmb, rcv, ml, mld, mls, mly, mlz, mlr, wsend, wrecv,
-                qsem, osem, ksem, vsem,
+                isem, wsem, qsem, osem, ksem, vsem,
                 d2d_s, d2d_r, a2a_s, a2a_r, mld_s, mld_r, mly_s, mly_r, mlz_s, mlz_r, wo_s, wo_r,
                 agz_s, agz_r, agy_s, agy_r, agc_s, agc_r):
     dp = lax.axis_index("dp")
@@ -63,6 +64,10 @@
     def cpeer(d):
         return (dp, ((chip + d) % 8) * 2 + core)
 
+    c_in = [pltpu.make_async_copy(src, dst, isem.at[i])
+            for i, (src, dst) in enumerate(((x_h, x_s), (g_h, g_s), (b_h, b_s), (freq_h, freq_s), (pos_h, pos)))]
+    c_up = pltpu.make_async_copy(wup, wu, wsem.at[0])
+    c_dn = pltpu.make_async_copy(wdn, wd, wsem.at[1])
     c_q = [pltpu.make_async_copy(wqkv.at[:, pl.ds(QCHUNK * i, QCHUNK)], wq.at[i % QSLOTS], qsem.at[i]) for i in range(NQ)]
 
     def c_kv(s):
@@ -76,7 +81,9 @@
 
     c_o = [pltpu.make_async_copy(wout.at[pl.ds((2 * core + i) * FF, FF)], (wu, wd)[i], osem.at[i]) for i in range(2)]
 
-    for i in range(QSLOTS):
+    for c in c_in + [c_up, c_dn]:
+        c.start()
+    for i in range(3):
         c_q[i].start()
 
     barrier = pltpu.get_barrier_semaphore()
@@ -84,28 +91,41 @@
     for d in range(1, GROUPS):
         pl.semaphore_signal(barrier, inc=1, device_id=cpeer(d), device_id_type=MESH)
 
+    for c in c_in:
+        c.wait()
+    gamma = g_s[...].reshape(1, D)
+    beta = b_s[...].reshape(1, D)
+
     def norm_rows(i, carry):
         rows = pl.ds(pl.multiple_of(16 * i, 16), 16)
-        xf = x_ref[rows, :].astype(F32)
+        xf = x_s[rows, :].astype(F32)
         cen = xf - jnp.mean(xf, axis=-1, keepdims=True)
         var = jnp.mean(cen * cen, axis=-1, keepdims=True)
-        h_s[rows, :] = (cen * lax.rsqrt(var + LN_EPS) * g_ref[...] + b_ref[...]).astype(BF16)
+        h_s[rows, :] = (cen * lax.rsqrt(var + LN_EPS) * gamma + beta).astype(BF16)
         return carry
 
     lax.fori_loop(0, ROWS // 16, norm_rows, 0)
 
-    up = lax.dot_general(h_s[...], wup[...], (((1,), (1,)), ((), ())), preferred_element_type=F32)
+    for b in range(ROWS):
+        posv[b:b + 1, :] = jnp.full((1, HD), pos[b], jnp.int32)
+    angles = posv[...].astype(F32) * freq_s[...]
+    cos = jnp.cos(angles)
+    sin = jnp.sin(angles)
+    sin = jnp.where(lax.broadcasted_iota(jnp.int32, (ROWS, HD), 1) < HD // 2, -sin, sin)
+
+    c_up.wait()
+    c_q[3].start()
+    up = lax.dot_general(h_s[...], wu[...], (((1,), (1,)), ((), ())), preferred_element_type=F32)
     act[...] = (0.5 * up * (1.0 + lax.erf(up * (1.0 / math.sqrt(2.0))))).astype(BF16)
+    c_dn.wait()
     for n in range(HALF):
-        part = jnp.dot(act[...], wdn[:, 256 * n:256 * (n + 1)], preferred_element_type=F32)
+        part = jnp.dot(act[...], wd[:, 256 * n:256 * (n + 1)], preferred_element_type=F32)
         for j in (2 * n, 2 * n + 1):
             ml[:, j // HALF, j % HALF] = part[:, 128 * (j - 2 * n):128 * (j - 2 * n + 1)].reshape(GROUPS, 8, HD)
     pl.semaphore_wait(barrier, GROUPS)
     r_mld = remote(ml.at[:, 1 - core], mld, mld_s, mld_r, partner)
     r_mld.start()
 
-    cos = cos_ref[...]
-    sin = sin_ref[...]
     r_mly = remote(mls.at[:, 1 - y], mly, mly_s, mly_r, ypeer)
     for ch in range(NQ):
         c_q[ch].wait()
@@ -131,33 +151,31 @@
             mls[...] = ml[:, core].reshape(4, 2, HALF, 8, HD) + mld[...].reshape(4, 2, HALF, 8, HD)
             r_mly.start()
 
-    row_id = lax.broadcasted_iota(jnp.int32, (SEQ, HD), 0)
     col_id = lax.broadcasted_iota(jnp.int32, (NH, SEQ), 1)
     sub = lax.broadcasted_iota(jnp.int32, (NH, HD), 0)
     lane = lax.broadcasted_iota(jnp.int32, (NH, HD), 1)
 
     def attend(s):
         p = (chip + s + 1) % 8
+        local = [pos[8 * p + r] - me * SEQ for r in range(8)]
+        inside = [(x >= 0) & (x < SEQ) for x in local]
+        qs = [q4[p, :, r, :] for r in range(8)]
+        scores = [lax.dot_general(qs[r].astype(BF16), ko[8 * p + r], (((1,), (1,)), ((), ())), preferred_element_type=F32)
+                  for r in range(8)]
+        s_new = [jnp.sum(qs[r] * kn[p, r:r + 1, :], axis=-1, keepdims=True) * HD ** -0.5 for r in range(8)]
+        s_new = [jnp.where(inside[r], s_new[r], NEG_FILL) for r in range(8)]
+        masked = [jnp.where(col_id < local[r], scores[r] * HD ** -0.5, NEG_FILL) for r in range(8)]
+        ms = [jnp.maximum(jnp.max(masked[r], axis=-1, keepdims=True), s_new[r]) for r in range(8)]
+        es = [jnp.where(col_id < local[r], jnp.exp(masked[r] - ms[r]), 0.0) for r in range(8)]
+        e_new = [jnp.where(inside[r], jnp.exp(s_new[r] - ms[r]), 0.0) for r in range(8)]
+        os = [jnp.dot(es[r].astype(BF16), vo[8 * p + r], preferred_element_type=F32) for r in range(8)]
+        ls = [jnp.sum(es[r], axis=-1, keepdims=True) + e_new[r] for r in range(8)]
         for r in range(8):
-            b = 8 * p + r
-            local = pos[b] - me * SEQ
-            here = row_id == local
-            kb = jnp.where(here, jnp.broadcast_to(kn[p, r:r + 1, :], (SEQ, HD)).astype(BF16), ko[b])
-            vb = jnp.where(here, jnp.broadcast_to(vn[p, r:r + 1, :], (SEQ, HD)).astype(BF16), vo[b])
-            ko[b] = kb
-            vo[b] = vb
-            q = q4[p, :, r, :].astype(BF16)
-            sc = lax.dot_general(q, kb, (((1,), (1,)), ((), ())), preferred_element_type=F32) * HD ** -0.5
-            valid = col_id <= local
-            sc = jnp.where(valid, sc, NEG_FILL)
-            m = jnp.max(sc, axis=-1, keepdims=True)
-            e = jnp.where(valid, jnp.exp(sc - m), 0.0)
-            l = jnp.sum(e, axis=-1, keepdims=True)
-            o = jnp.dot(e.astype(BF16), vb, preferred_element_type=F32)
+            o = os[r] + e_new[r].astype(BF16).astype(F32) * vn[p, r:r + 1, :]
             for half in range(2):
                 idx = sub - HALF * half
                 own = (idx >= 0) & (idx < HALF)
-                t = jnp.where(own & (lane == idx), m, jnp.where(own & (lane == idx + LANE_L), l, 0.0))
+                t = jnp.where(own & (lane == idx), ms[r], jnp.where(own & (lane == idx + LANE_L), ls[r], 0.0))
                 st[s, half, HALF, r:r + 1, :] = jnp.sum(t, axis=0, keepdims=True)
                 st[s, half, 0:HALF, r, :] = o[HALF * half:HALF * (half + 1), :]
 
@@ -198,7 +216,7 @@
         def _():
             c_o[1].start()
 
-        @pl.when(s == 1)
+        @pl.when(s == 4)
         def _():
             r_mly.wait_recv()
             mlz[...] = mls[:, y] + mly[...]
@@ -300,14 +318,27 @@
         send_c(d, 1).wait_send()
 
 
-def write_kernel(ko, vo, agb, x_ref, out_ref, k_out, v_out, sem):
+def write_kernel(pos, ko, vo, kn, vn, agb, x_ref, out_ref, k_out, v_out, kw, vw, sem):
+    me = lax.axis_index("sp")
+    sub = lax.broadcasted_iota(jnp.int32, (16, HD), 0)
     copies = []
-    for i in range(8):
+    for i in range(GROUPS):
+        for r in range(8):
+            b = 8 * i + r
+            local = pos[b] - me * SEQ
+
+            @pl.when((local >= 0) & (local < SEQ))
+            def _():
+                tile = pl.ds(pl.multiple_of(local // 16 * 16, 16), 16)
+                here = sub == local % 16
+                kw[b, tile, :] = jnp.where(here, kn[i, r:r + 1, :], ko[b, tile, :].astype(F32)).astype(BF16)
+                vw[b, tile, :] = jnp.where(here, vn[i, r:r + 1, :], vo[b, tile, :].astype(F32)).astype(BF16)
+
         rows = pl.ds(8 * i, 8)
-        copies.append(pltpu.make_async_copy(ko.at[rows], k_out.at[rows], sem.at[2 * i]))
-        copies.append(pltpu.make_async_copy(vo.at[rows], v_out.at[rows], sem.at[2 * i + 1]))
-    for c in copies:
-        c.start()
+        copies.append(pltpu.make_async_copy(kw.at[rows], k_out.at[rows], sem.at[2 * i]))
+        copies.append(pltpu.make_async_copy(vw.at[rows], v_out.at[rows], sem.at[2 * i + 1]))
+        copies[-2].start()
+        copies[-1].start()
     for q in range(GROUPS // 2):
         rows = slice(16 * q, 16 * (q + 1))
         for j in range(NH):
@@ -318,35 +349,45 @@
         c.wait()
 
 
+def in_hbm(array):
+    return pltpu.with_memory_space_constraint(array, pltpu.HBM)
+
+
+def in_vmem(array):
+    return pltpu.with_memory_space_constraint(array, pltpu.VMEM)
+
+
 def device_step(hidden, ln_gamma, ln_beta, w_qkv, w_out, w_up, w_down, k_cache, v_cache, positions):
-    inv_freq = 1.0 / (ROPE_BASE ** (jnp.arange(0, HD, 2, dtype=F32) / HD))
-    angles = positions.astype(F32)[:, None] * inv_freq[None, :]
-    cos, sin = jnp.cos(angles), jnp.sin(angles)
-    cos_full = jnp.concatenate([cos, cos], axis=-1)
-    sin_signed = jnp.concatenate([-sin, sin], axis=-1)
+    pair_ids = np.arange(0, HD, 2, dtype=np.float64) / HD
+    freq = jnp.asarray(np.tile(ROPE_BASE ** -pair_ids, 2)[None], F32)
 
     vmem = pl.BlockSpec(memory_space=pltpu.VMEM)
     hbm = pl.BlockSpec(memory_space=pltpu.HBM)
-    smem = pl.BlockSpec(memory_space=pltpu.SMEM)
     dma = pltpu.SemaphoreType.DMA
-    agb, k_new, v_new = pl.pallas_call(
+    agb, k_blk, v_blk, k_row, v_row = pl.pallas_call(
         main_kernel,
         out_shape=(
-            jax.ShapeDtypeStruct((GROUPS, 2, HALF, 8, HD), F32),
-            jax.ShapeDtypeStruct(k_cache.shape, BF16),
-            jax.ShapeDtypeStruct(v_cache.shape, BF16),
+            pltpu.VMEM((GROUPS, 2, HALF, 8, HD), F32),
+            pltpu.VMEM(k_cache.shape, BF16),
+            pltpu.VMEM(v_cache.shape, BF16),
+            pltpu.VMEM((GROUPS, 8, HD), F32),
+            pltpu.VMEM((GROUPS, 8, HD), F32),
         ),
-        in_specs=[smem] + [vmem] * 5 + [hbm] * 2 + [vmem] * 2 + [hbm] * 2,
-        out_specs=(vmem, vmem, vmem),
+        in_specs=[hbm] * 11,
+        out_specs=(vmem,) * 5,
         scratch_shapes=[
+            pltpu.SMEM((ROWS,), jnp.int32),
+            pltpu.VMEM((ROWS, D), BF16),
+            pltpu.VMEM((D,), F32),
+            pltpu.VMEM((D,), F32),
+            pltpu.VMEM((1, HD), F32),
+            pltpu.VMEM((ROWS, HD), jnp.int32),
             pltpu.VMEM((QSLOTS, D, QCHUNK), BF16),
             pltpu.VMEM((FF, D), BF16),
             pltpu.VMEM((FF, D), BF16),
             pltpu.VMEM((ROWS, D), BF16),
             pltpu.VMEM((ROWS, FF), BF16),
             pltpu.VMEM((GROUPS, NH, 8, HD), F32),
-            pltpu.VMEM((GROUPS, 8, HD), F32),
-            pltpu.VMEM((GROUPS, 8, HD), F32),
             pltpu.VMEM((GROUPS, 2, HALF + 1, 8, HD), F32),
             pltpu.VMEM((GROUPS, HALF + 1, 8, HD), F32),
             pltpu.VMEM((GROUPS, HALF + 1, 8, HD), F32),
@@ -359,29 +400,33 @@
             pltpu.VMEM((3, HALF, 8, HD), F32),
             pltpu.VMEM((HALF, 8, HD), F32),
             pltpu.VMEM((HALF, 8, HD), F32),
-            dma((NQ,)), dma((2,)), dma((GROUPS,)), dma((GROUPS,)),
+            dma((5,)), dma((2,)), dma((NQ,)), dma((2,)), dma((GROUPS,)), dma((GROUPS,)),
             dma((GROUPS,)), dma((GROUPS,)), dma((GROUPS - 1,)), dma((GROUPS - 1,)),
             dma, dma, dma, dma, dma((3,)), dma((3,)), dma, dma,
             dma((3,)), dma((3,)), dma((4,)), dma((4,)), dma((8,)), dma((8,)),
         ],
-        compiler_params=pltpu.CompilerParams(collective_id=0, has_side_effects=True, vmem_limit_bytes=28 * 2**20),
+        compiler_params=pltpu.CompilerParams(collective_id=0, has_side_effects=True, vmem_limit_bytes=32 * 2**20),
         name="layer",
-    )(positions, hidden, ln_gamma.reshape(1, D), ln_beta.reshape(1, D), cos_full, sin_signed,
-      w_qkv, w_out, w_up.T, w_down, k_cache, v_cache)
-
-    return pl.pallas_call(
+    )(*[in_hbm(a) for a in (positions, hidden, ln_gamma, ln_beta, freq,
+                               w_qkv, w_out, w_up.T, w_down, k_cache, v_cache)])
+
+    out, k_new, v_new, _, _ = pl.pallas_call(
         write_kernel,
         out_shape=(
             jax.ShapeDtypeStruct(hidden.shape, BF16),
             jax.ShapeDtypeStruct(k_cache.shape, BF16),
             jax.ShapeDtypeStruct(v_cache.shape, BF16),
+            pltpu.VMEM(k_cache.shape, BF16),
+            pltpu.VMEM(v_cache.shape, BF16),
         ),
-        in_specs=[vmem] * 4,
-        out_specs=(vmem, hbm, hbm),
-        scratch_shapes=[dma((16,))],
+        in_specs=[pl.BlockSpec(memory_space=pltpu.SMEM)] + [vmem] * 6,
+        out_specs=(vmem, hbm, hbm, vmem, vmem),
+        scratch_shapes=[dma((2 * GROUPS,))],
+        input_output_aliases={1: 3, 2: 4},
         compiler_params=pltpu.CompilerParams(vmem_limit_bytes=16 * 2**20),
         name="write",
-    )(k_new, v_new, agb, hidden)
+    )(positions, *[in_vmem(a) for a in (k_blk, v_blk, k_row, v_row, agb)], hidden)
+    return out, k_new, v_new
 
 
 def solution(mesh):

time: 64.2 us -> 52.2 us (0.81)
  local copies, waits for them, and re-layouts: 7.31 us -> 0.01 us
  Pallas kernels: 54.9 us -> 51.4 us
  other arithmetic: 0.95 us -> 0 us
    unnamed x8 -> x4, local copies, waits for them, and re-layouts: 5.88 us -> 0.01 us
    pallas_call x1, Pallas kernels: 48.2 us -> 44.1 us  [device_step(): pl.pallas_call(main_kernel, out_shape=(pltpu.VMEM((GROUPS, 2, HALF, 8, HD...]
    reshape x2 -> x0, local copies, waits for them, and re-layouts: 1.43 us -> none  [the longest x1 0.72 us: device_step(): ln_gamma.reshape(1, D)]
    convert_element_type x1 -> x0, other arithmetic: 0.66 us -> none  [device_step(): angles = positions.astype(F32)[:, None] * inv_freq[None, :]]
where the time goes in v2:
time: 52.2 us; the launch traced here: 52.1 us
  Pallas kernels  51.4 us (98%)
  between operations  0.67 us (1%)
    pallas_call x1, Pallas kernels, device_step(): pl.pallas_call(main_kernel, out_shape=(pltpu.VMEM((GROUPS, 2, HALF, 8, HD...  44.1 us
    pallas_call x1, Pallas kernels, device_step(): pl.pallas_call(write_kernel, out_shape=(jax.ShapeDtypeStruct(hidden.shape...  7.32 us

profile of v2, /device:TPU:0, one launch (start us, length us, event | category | flops | bytes accessed | tf_op | source)
XLA Modules:
  0.0 52.1 jit_solution(10912880280974433308)
XLA Ops:
  0.6 0.0 copy-start
  0.6 0.0 copy-start.1
  0.7 44.1 %layer.1 = (f32[8,2,11,8,128]{4,3,2,1,0:T(8,128)S(1)}, bf16[64,512,128]{2,1,0:T(8,128)(2,1)S(1)}, bf16[64,512,128]{2,1,0:T(8,128)(2,1)S(1)}, f32[8,8,128]{2,1,0:T(8,128)S(1)}, f32[8,8,128]{2,1,0:T(8,128)S(1)}) custom-call(s32[64]{0:T(128)} %pos.1, bf16[64,2816]{1,0:T(8,128)(2,1)} %x_ref.1, f32[2816]{0:T(1024)} %g_h.1, f32[2816]{0:T(1024)} %b_h.1, ...), custom_call_target="tpu_custom_call" | custom-call | tf_op jit(solution)/shard_map/layer/pallas_call | solution.py:367
  44.8 0.0 copy-done
  44.8 0.0 copy-done.1
  44.8 7.3 %write.1 = (bf16[64,2816]{1,0:T(8,128)(2,1)}, bf16[64,512,128]{2,1,0:T(8,128)(2,1)}, bf16[64,512,128]{2,1,0:T(8,128)(2,1)}, bf16[64,512,128]{2,1,0:T(8,128)(2,1)S(1)}, bf16[64,512,128]{2,1,0:T(8,128)(2,1)S(1)}) custom-call(s32[64]{0:T(128)S(1)} %copy-done.1, ...), custom_call_target="tpu_custom_call", output_to_operand_aliasing={{3}: (1, {}), {4}: (2, {})} | custom-call | tf_op jit(solution)/shard_map/write/pallas_call | solution.py:413
Async XLA Ops:
  0.6 44.1 %copy-start = (bf16[64,2816]{1,0:T(8,128)(2,1)S(1)}, bf16[64,2816]{1,0:T(8,128)(2,1)}, u32[]{:S(2)}) copy-start(bf16[64,2816]{1,0:T(8,128)(2,1)} %x_ref.1) | copy-start | bytes 1081348
  0.6 44.1 %copy-start.1 = (s32[64]{0:T(128)S(1)}, s32[64]{0:T(128)}, u32[]{:S(2)}) copy-start(s32[64]{0:T(128)} %pos.1) | copy-start | bytes 772

commit v3 on v2

--- a/solution.py
+++ b/solution.py
@@ -45,9 +45,9 @@
 def main_kernel(pos_h, x_h, g_h, b_h, freq_h, wqkv, wout, wup, wdn, kh, vh,
                 agb, ko, vo, kn, vn,
                 pos, x_s, g_s, b_s, freq_s, posv, wq, wu, wd, h_s, act, q4,
-                st, d2d, cmb, rcv, ml, mld, mls, mly, mlz, mlr, wsend, wrecv,
+                st, d2d, cmb, yrcv, zsnd, zrcv, ml, mld, mls, mly, mlz, mlr, wsend, wrecv,
                 isem, wsem, qsem, osem, ksem, vsem,
-                d2d_s, d2d_r, a2a_s, a2a_r, mld_s, mld_r, mly_s, mly_r, mlz_s, mlz_r, wo_s, wo_r,
+                d2d_s, d2d_r, sty_s, sty_r, stz_s, stz_r, mld_s, mld_r, mly_s, mly_r, mlz_s, mlz_r, wo_s, wo_r,
                 agz_s, agz_r, agy_s, agy_r, agc_s, agc_r):
     dp = lax.axis_index("dp")
     me = lax.axis_index("sp")
@@ -61,17 +61,17 @@
     def zpeer(d):
         return (dp, ((z + d) % 4) * 4 + y * 2 + core)
 
-    def cpeer(d):
-        return (dp, ((chip + d) % 8) * 2 + core)
-
     c_in = [pltpu.make_async_copy(src, dst, isem.at[i])
             for i, (src, dst) in enumerate(((x_h, x_s), (g_h, g_s), (b_h, b_s), (freq_h, freq_s), (pos_h, pos)))]
     c_up = pltpu.make_async_copy(wup, wu, wsem.at[0])
     c_dn = pltpu.make_async_copy(wdn, wd, wsem.at[1])
     c_q = [pltpu.make_async_copy(wqkv.at[:, pl.ds(QCHUNK * i, QCHUNK)], wq.at[i % QSLOTS], qsem.at[i]) for i in range(NQ)]
 
+    def group(s):
+        return ((z + s // 2 + 1) % 4) * 2 + (y + s + 1) % 2
+
     def c_kv(s):
-        rows = pl.ds(8 * ((chip + s + 1) % 8), 8)
+        rows = pl.ds(8 * group(s), 8)
         return (pltpu.make_async_copy(kh.at[rows], ko.at[rows], ksem.at[s]),
                 pltpu.make_async_copy(vh.at[rows], vo.at[rows], vsem.at[s]))
 
@@ -88,8 +88,9 @@
 
     barrier = pltpu.get_barrier_semaphore()
     pl.semaphore_signal(barrier, inc=1, device_id=partner, device_id_type=MESH)
-    for d in range(1, GROUPS):
-        pl.semaphore_signal(barrier, inc=1, device_id=cpeer(d), device_id_type=MESH)
+    pl.semaphore_signal(barrier, inc=1, device_id=ypeer, device_id_type=MESH)
+    for d in range(1, 4):
+        pl.semaphore_signal(barrier, inc=1, device_id=zpeer(d), device_id_type=MESH)
 
     for c in c_in:
         c.wait()
@@ -122,11 +123,22 @@
         part = jnp.dot(act[...], wd[:, 256 * n:256 * (n + 1)], preferred_element_type=F32)
         for j in (2 * n, 2 * n + 1):
             ml[:, j // HALF, j % HALF] = part[:, 128 * (j - 2 * n):128 * (j - 2 * n + 1)].reshape(GROUPS, 8, HD)
-    pl.semaphore_wait(barrier, GROUPS)
+    pl.semaphore_wait(barrier, 5)
     r_mld = remote(ml.at[:, 1 - core], mld, mld_s, mld_r, partner)
     r_mld.start()
 
-    r_mly = remote(mls.at[:, 1 - y], mly, mly_s, mly_r, ypeer)
+
+    def r_mly(j):
+        zt = (z + j + 1) % 4
+        return remote(mls.at[zt, 1 - y], mly.at[j], mly_s.at[j], mly_r.at[j], ypeer)
+
+    def r_mlz(j):
+        return remote(mlz.at[j], mlr.at[j], mlz_s.at[j], mlz_r.at[j], zpeer(j + 1))
+
+    def mlp_z(j):
+        r_mly(j).wait_recv()
+        mlz[j] = mls[(z + j + 1) % 4, y] + mly[j]
+
     for ch in range(NQ):
         c_q[ch].wait()
         acc = jnp.dot(h_s[...], wq[ch % QSLOTS], preferred_element_type=F32).astype(BF16).astype(F32)
@@ -146,17 +158,18 @@
                 kn[...] = vec
             else:
                 vn[...] = vec
-        if ch == 2:
+        if ch == 1:
             r_mld.wait_recv()
             mls[...] = ml[:, core].reshape(4, 2, HALF, 8, HD) + mld[...].reshape(4, 2, HALF, 8, HD)
-            r_mly.start()
+            for j in range(4):
+                r_mly(j).start()
 
     col_id = lax.broadcasted_iota(jnp.int32, (NH, SEQ), 1)
     sub = lax.broadcasted_iota(jnp.int32, (NH, HD), 0)
     lane = lax.broadcasted_iota(jnp.int32, (NH, HD), 1)
 
     def attend(s):
-        p = (chip + s + 1) % 8
+        p = group(s)
         local = [pos[8 * p + r] - me * SEQ for r in range(8)]
         inside = [(x >= 0) & (x < SEQ) for x in local]
         qs = [q4[p, :, r, :] for r in range(8)]
@@ -182,22 +195,30 @@
     def r_d2d(s):
         return remote(st.at[s, 1 - core], d2d.at[s], d2d_s.at[s], d2d_r.at[s], partner)
 
-    def r_a2a(s):
-        return remote(cmb.at[s], rcv.at[s], a2a_s.at[s], a2a_r.at[s], cpeer(s + 1))
+    def r_y(j):
+        return remote(cmb.at[2 * j], yrcv.at[j], sty_s.at[j], sty_r.at[j], ypeer)
+
+    def r_z(j):
+        return remote(zsnd.at[j], zrcv.at[j], stz_s.at[j], stz_r.at[j], zpeer(j + 1))
 
     lane8 = lax.broadcasted_iota(jnp.int32, (8, HD), 1)
 
-    def pair(s):
-        r_d2d(s).wait_recv()
-        ta, tb = st[s, core, HALF], d2d[s, HALF]
+    def merge(dst, a, b):
+        ta, tb = a[HALF], b[HALF]
         top = jnp.maximum(ta, tb)
         wa, wb = weights_of(ta, top), weights_of(tb, top)
         total = ta * pltpu.roll(wa, LANE_L, 1) + tb * pltpu.roll(wb, LANE_L, 1)
-        cmb[s, HALF] = jnp.where(lane8 < LANE_L, top, total)
+        dst[HALF] = jnp.where(lane8 < LANE_L, top, total)
         for i in range(HALF):
-            cmb[s, i] = st[s, core, i] * wa[:, i:i + 1] + d2d[s, i] * wb[:, i:i + 1]
-
-    r_mlz = [remote(mlz.at[(z + d) % 4], mlr.at[d - 1], mlz_s.at[d - 1], mlz_r.at[d - 1], zpeer(d)) for d in range(1, 4)]
+            dst[i] = a[i] * wa[:, i:i + 1] + b[i] * wb[:, i:i + 1]
+
+    def pair(s):
+        r_d2d(s).wait_recv()
+        merge(cmb.at[s], st.at[s, core], d2d.at[s])
+
+    def pair_y(j):
+        r_y(j).wait_recv()
+        merge(zsnd.at[j], cmb.at[2 * j + 1], yrcv.at[j])
 
     def step(s, carry):
         ck, cv = c_kv(s)
@@ -216,41 +237,46 @@
         def _():
             c_o[1].start()
 
-        @pl.when(s == 4)
-        def _():
-            r_mly.wait_recv()
-            mlz[...] = mls[:, y] + mly[...]
-            for c in r_mlz:
-                c.start()
-
         attend(s)
         r_d2d(s).start()
 
         @pl.when(s > 0)
         def _():
             pair(s - 1)
-            r_a2a(s - 1).start()
+
+        @pl.when(s % 2 == 1)
+        def _():
+            r_y(s // 2).start()
+
+        @pl.when((s >= 2) & (s < 5))
+        def _():
+            mlp_z(s - 2)
+            r_mlz(s - 2).start()
+
+        @pl.when((s == 5) | (s == 7))
+        def _():
+            pair_y((s - 5) // 2)
+            r_z((s - 5) // 2).start()
 
         return carry
 
     lax.fori_loop(0, GROUPS, step, 0)
     pair(GROUPS - 1)
-
-    for c in r_mlz:
-        c.wait_recv()
-    fin = mlz[z] + mlr[0] + mlr[1] + mlr[2]
-
-    for s in range(GROUPS - 1):
-        r_a2a(s).wait_recv()
-    tiles = [cmb[GROUPS - 1, HALF]] + [rcv[s, HALF] for s in range(GROUPS - 1)]
+    pair_y(2)
+    r_z(2).start()
+
+    mlp_z(3)
+    pair_y(3)
+    for j in range(3):
+        r_z(j).wait_recv()
+    parts = [zsnd.at[3], zrcv.at[0], zrcv.at[1], zrcv.at[2]]
+    tiles = [part[HALF] for part in parts]
     top = functools.reduce(jnp.maximum, tiles)
     ws = [weights_of(t, top) for t in tiles]
     total = functools.reduce(jnp.add, [t * pltpu.roll(w, LANE_L, 1) for t, w in zip(tiles, ws)])
     heads = []
     for i in range(HALF):
-        acc = cmb[GROUPS - 1, i] * ws[0][:, i:i + 1]
-        for s in range(GROUPS - 1):
-            acc += rcv[s, i] * ws[s + 1][:, i:i + 1]
+        acc = functools.reduce(jnp.add, [part[i] * w[:, i:i + 1] for part, w in zip(parts, ws)])
         heads.append((acc / total[:, LANE_L + i:LANE_L + i + 1]).astype(BF16))
     ctx = jnp.concatenate(heads, axis=1)
 
@@ -267,6 +293,9 @@
     r_wo = remote(wsend, wrecv, wo_s, wo_r, partner)
     r_wo.start()
     mine = project(core)
+    for j in range(3):
+        r_mlz(j).wait_recv()
+    fin = mlz[3] + mlr[0] + mlr[1] + mlr[2]
     r_wo.wait_recv()
     for i in range(HALF):
         agb[chip, core, i] = mine[:, HD * i:HD * (i + 1)] + wrecv[i] + fin[i]
@@ -286,29 +315,36 @@
         yy = (y + other_y) % 2
         return remote(piece(zz, yy), piece(zz, yy), agc_s.at[2 * d + other_y], agc_r.at[2 * d + other_y], partner)
 
-    for d in (2, 1, 3):
-        send_z(d).start()
+    flip = z // 2
+    near = z + flip * (3 - 2 * z)
+    order = [src + flip * (3 - 2 * src) for src in (1 - near, 2, 3)]
+    dist = [(z + 4 - src) % 4 for src in order]
+    for i in (2, 1, 0):
+        send_z((order[i] + 4 - z) % 4).start()
     send_y(0).start()
     send_c(0, 0).start()
-    for d in (1, 2, 3):
-        send_z(d).wait_recv()
-        send_y(d).start()
-        send_c(d, 0).start()
-    for d in range(4):
-        send_y(d).wait_recv()
-        send_c(d, 1).start()
+    for i in range(3):
+        send_z(dist[i]).wait_recv()
+        send_y(dist[i]).start()
+        send_c(dist[i], 0).start()
+        back = 0 if i == 0 else dist[i - 1]
+        send_y(back).wait_recv()
+        send_c(back, 1).start()
+    send_y(dist[2]).wait_recv()
+    send_c(dist[2], 1).start()
     for d in range(4):
         for o in range(2):
             send_c(d, o).wait_recv()
 
     r_mld.wait_send()
-    r_mly.wait_send()
-    for c in r_mlz:
-        c.wait_send()
     for s in range(GROUPS):
         r_d2d(s).wait_send()
-    for s in range(GROUPS - 1):
-        r_a2a(s).wait_send()
+    for j in range(4):
+        r_mly(j).wait_send()
+        r_y(j).wait_send()
+    for j in range(3):
+        r_mlz(j).wait_send()
+        r_z(j).wait_send()
     r_wo.wait_send()
     for d in (1, 2, 3):
         send_z(d).wait_send()
@@ -391,7 +427,9 @@
             pltpu.VMEM((GROUPS, 2, HALF + 1, 8, HD), F32),
             pltpu.VMEM((GROUPS, HALF + 1, 8, HD), F32),
             pltpu.VMEM((GROUPS, HALF + 1, 8, HD), F32),
-            pltpu.VMEM((GROUPS - 1, HALF + 1, 8, HD), F32),
+            pltpu.VMEM((4, HALF + 1, 8, HD), F32),
+            pltpu.VMEM((4, HALF + 1, 8, HD), F32),
+            pltpu.VMEM((3, HALF + 1, 8, HD), F32),
             pltpu.VMEM((GROUPS, 2, HALF, 8, HD), F32),
             pltpu.VMEM((GROUPS, HALF, 8, HD), F32),
             pltpu.VMEM((4, 2, HALF, 8, HD), F32),
@@ -401,8 +439,8 @@
             pltpu.VMEM((HALF, 8, HD), F32),
             pltpu.VMEM((HALF, 8, HD), F32),
             dma((5,)), dma((2,)), dma((NQ,)), dma((2,)), dma((GROUPS,)), dma((GROUPS,)),
-            dma((GROUPS,)), dma((GROUPS,)), dma((GROUPS - 1,)), dma((GROUPS - 1,)),
-            dma, dma, dma, dma, dma((3,)), dma((3,)), dma, dma,
+            dma((GROUPS,)), dma((GROUPS,)), dma((4,)), dma((4,)), dma((3,)), dma((3,)),
+            dma, dma, dma((4,)), dma((4,)), dma((3,)), dma((3,)), dma, dma,
             dma((3,)), dma((3,)), dma((4,)), dma((4,)), dma((8,)), dma((8,)),
         ],
         compiler_params=pltpu.CompilerParams(collective_id=0, has_side_effects=True, vmem_limit_bytes=32 * 2**20),

time: 52.2 us -> 49.7 us (0.952)
  Pallas kernels: 51.4 us -> 48.8 us
    pallas_call x1, Pallas kernels: 44.1 us -> 41.5 us  [device_step(): pl.pallas_call(main_kernel, out_shape=(pltpu.VMEM((GROUPS, 2, HALF, 8, HD...]
where the time goes in v3:
time: 49.7 us; the launch traced here: 49.5 us
  Pallas kernels  48.8 us (98%)
  between operations  0.67 us (1%)
    pallas_call x1, Pallas kernels, device_step(): pl.pallas_call(main_kernel, out_shape=(pltpu.VMEM((GROUPS, 2, HALF, 8, HD...  41.5 us
    pallas_call x1, Pallas kernels, device_step(): pl.pallas_call(write_kernel, out_shape=(jax.ShapeDtypeStruct(hidden.shape...  7.32 us

profile of v3, /device:TPU:0, one launch (start us, length us, event | category | flops | bytes accessed | tf_op | source)
XLA Modules:
  0.0 49.5 jit_solution(16742713877898892254)
XLA Ops:
  0.6 0.0 copy-start
  0.6 0.0 copy-start.1
  0.7 41.5 %layer.1 = (f32[8,2,11,8,128]{4,3,2,1,0:T(8,128)S(1)}, bf16[64,512,128]{2,1,0:T(8,128)(2,1)S(1)}, bf16[64,512,128]{2,1,0:T(8,128)(2,1)S(1)}, f32[8,8,128]{2,1,0:T(8,128)S(1)}, f32[8,8,128]{2,1,0:T(8,128)S(1)}) custom-call(s32[64]{0:T(128)} %pos.1, bf16[64,2816]{1,0:T(8,128)(2,1)} %x_ref.1, f32[2816]{0:T(1024)} %g_h.1, f32[2816]{0:T(1024)} %b_h.1, ...), custom_call_target="tpu_custom_call" | custom-call | tf_op jit(solution)/shard_map/layer/pallas_call | solution.py:403
  42.2 0.0 copy-done
  42.2 0.0 copy-done.1
  42.2 7.3 %write.1 = (bf16[64,2816]{1,0:T(8,128)(2,1)}, bf16[64,512,128]{2,1,0:T(8,128)(2,1)}, bf16[64,512,128]{2,1,0:T(8,128)(2,1)}, bf16[64,512,128]{2,1,0:T(8,128)(2,1)S(1)}, bf16[64,512,128]{2,1,0:T(8,128)(2,1)S(1)}) custom-call(s32[64]{0:T(128)S(1)} %copy-done.1, ...), custom_call_target="tpu_custom_call", output_to_operand_aliasing={{3}: (1, {}), {4}: (2, {})} | custom-call | tf_op jit(solution)/shard_map/write/pallas_call | solution.py:451
Async XLA Ops:
  0.6 41.6 %copy-start = (bf16[64,2816]{1,0:T(8,128)(2,1)S(1)}, bf16[64,2816]{1,0:T(8,128)(2,1)}, u32[]{:S(2)}) copy-start(bf16[64,2816]{1,0:T(8,128)(2,1)} %x_ref.1) | copy-start | bytes 1081348
  0.6 41.6 %copy-start.1 = (s32[64]{0:T(128)S(1)}, s32[64]{0:T(128)}, u32[]{:S(2)}) copy-start(s32[64]{0:T(128)} %pos.1) | copy-start | bytes 772

commit v4 on v3

--- a/solution.py
+++ b/solution.py
@@ -68,7 +68,7 @@
     c_q = [pltpu.make_async_copy(wqkv.at[:, pl.ds(QCHUNK * i, QCHUNK)], wq.at[i % QSLOTS], qsem.at[i]) for i in range(NQ)]
 
     def group(s):
-        return ((z + s // 2 + 1) % 4) * 2 + (y + s + 1) % 2
+        return ((z + s + 1) % 4) * 2 + (y + s // 4 + 1) % 2
 
     def c_kv(s):
         rows = pl.ds(8 * group(s), 8)
@@ -92,7 +92,7 @@
     for d in range(1, 4):
         pl.semaphore_signal(barrier, inc=1, device_id=zpeer(d), device_id_type=MESH)
 
-    for c in c_in:
+    for c in c_in[:3]:
         c.wait()
     gamma = g_s[...].reshape(1, D)
     beta = b_s[...].reshape(1, D)
@@ -107,6 +107,8 @@
 
     lax.fori_loop(0, ROWS // 16, norm_rows, 0)
 
+    for c in c_in[3:]:
+        c.wait()
     for b in range(ROWS):
         posv[b:b + 1, :] = jnp.full((1, HD), pos[b], jnp.int32)
     angles = posv[...].astype(F32) * freq_s[...]
@@ -119,13 +121,18 @@
     up = lax.dot_general(h_s[...], wu[...], (((1,), (1,)), ((), ())), preferred_element_type=F32)
     act[...] = (0.5 * up * (1.0 + lax.erf(up * (1.0 / math.sqrt(2.0))))).astype(BF16)
     c_dn.wait()
-    for n in range(HALF):
-        part = jnp.dot(act[...], wd[:, 256 * n:256 * (n + 1)], preferred_element_type=F32)
-        for j in (2 * n, 2 * n + 1):
-            ml[:, j // HALF, j % HALF] = part[:, 128 * (j - 2 * n):128 * (j - 2 * n + 1)].reshape(GROUPS, 8, HD)
+
+    def down(column_half, dst):
+        cols = pl.ds(pl.multiple_of(HALF * HD * column_half, HD), HALF * HD)
+        part = jnp.dot(act[...], wd[:, cols], preferred_element_type=F32)
+        for j in range(HALF):
+            dst[:, j] = part[:, HD * j:HD * (j + 1)].reshape(GROUPS, 8, HD)
+
+    down(1 - core, ml.at[0])
     pl.semaphore_wait(barrier, 5)
-    r_mld = remote(ml.at[:, 1 - core], mld, mld_s, mld_r, partner)
+    r_mld = remote(ml.at[0], mld, mld_s, mld_r, partner)
     r_mld.start()
+    down(core, ml.at[1])
 
 
     def r_mly(j):
@@ -160,7 +167,7 @@
                 vn[...] = vec
         if ch == 1:
             r_mld.wait_recv()
-            mls[...] = ml[:, core].reshape(4, 2, HALF, 8, HD) + mld[...].reshape(4, 2, HALF, 8, HD)
+            mls[...] = ml[1].reshape(4, 2, HALF, 8, HD) + mld[...].reshape(4, 2, HALF, 8, HD)
             for j in range(4):
                 r_mly(j).start()
 
@@ -196,7 +203,7 @@
         return remote(st.at[s, 1 - core], d2d.at[s], d2d_s.at[s], d2d_r.at[s], partner)
 
     def r_y(j):
-        return remote(cmb.at[2 * j], yrcv.at[j], sty_s.at[j], sty_r.at[j], ypeer)
+        return remote(cmb.at[j], yrcv.at[j], sty_s.at[j], sty_r.at[j], ypeer)
 
     def r_z(j):
         return remote(zsnd.at[j], zrcv.at[j], stz_s.at[j], stz_r.at[j], zpeer(j + 1))
@@ -218,7 +225,7 @@
 
     def pair_y(j):
         r_y(j).wait_recv()
-        merge(zsnd.at[j], cmb.at[2 * j + 1], yrcv.at[j])
+        merge(zsnd.at[j], cmb.at[4 + j], yrcv.at[j])
 
     def step(s, carry):
         ck, cv = c_kv(s)
@@ -244,28 +251,25 @@
         def _():
             pair(s - 1)
 
-        @pl.when(s % 2 == 1)
-        def _():
-            r_y(s // 2).start()
-
-        @pl.when((s >= 2) & (s < 5))
-        def _():
-            mlp_z(s - 2)
-            r_mlz(s - 2).start()
-
-        @pl.when((s == 5) | (s == 7))
-        def _():
-            pair_y((s - 5) // 2)
-            r_z((s - 5) // 2).start()
+        @pl.when((s >= 1) & (s < 5))
+        def _():
+            r_y(s - 1).start()
+
+        @pl.when((s >= 1) & (s < 4))
+        def _():
+            mlp_z(s - 1)
+            r_mlz(s - 1).start()
+
+        @pl.when(s >= 5)
+        def _():
+            pair_y(s - 5)
+            r_z(s - 5).start()
 
         return carry
 
     lax.fori_loop(0, GROUPS, step, 0)
+    mlp_z(3)
     pair(GROUPS - 1)
-    pair_y(2)
-    r_z(2).start()
-
-    mlp_z(3)
     pair_y(3)
     for j in range(3):
         r_z(j).wait_recv()
@@ -323,15 +327,13 @@
         send_z((order[i] + 4 - z) % 4).start()
     send_y(0).start()
     send_c(0, 0).start()
-    for i in range(3):
-        send_z(dist[i]).wait_recv()
-        send_y(dist[i]).start()
-        send_c(dist[i], 0).start()
-        back = 0 if i == 0 else dist[i - 1]
-        send_y(back).wait_recv()
-        send_c(back, 1).start()
-    send_y(dist[2]).wait_recv()
-    send_c(dist[2], 1).start()
+    for d in dist:
+        send_z(d).wait_recv()
+        send_y(d).start()
+        send_c(d, 0).start()
+    for d in [0] + dist:
+        send_y(d).wait_recv()
+        send_c(d, 1).start()
     for d in range(4):
         for o in range(2):
             send_c(d, o).wait_recv()
@@ -354,7 +356,7 @@
         send_c(d, 1).wait_send()
 
 
-def write_kernel(pos, ko, vo, kn, vn, agb, x_ref, out_ref, k_out, v_out, kw, vw, sem):
+def write_kernel(pos, ko, vo, kn, vn, agb, x_ref, out, k_out, v_out, kw, vw, out_ref, sem):
     me = lax.axis_index("sp")
     sub = lax.broadcasted_iota(jnp.int32, (16, HD), 0)
     copies = []
@@ -381,6 +383,8 @@
             cols = slice(HD * j, HD * (j + 1))
             both = agb[2 * q:2 * q + 2, j // HALF, j % HALF].reshape(16, HD)
             out_ref[rows, cols] = (x_ref[rows, cols].astype(F32) + both).astype(BF16)
+    copies.append(pltpu.make_async_copy(out_ref, out, sem.at[2 * GROUPS]))
+    copies[-1].start()
     for c in copies:
         c.wait()
 
@@ -430,7 +434,7 @@
             pltpu.VMEM((4, HALF + 1, 8, HD), F32),
             pltpu.VMEM((4, HALF + 1, 8, HD), F32),
             pltpu.VMEM((3, HALF + 1, 8, HD), F32),
-            pltpu.VMEM((GROUPS, 2, HALF, 8, HD), F32),
+            pltpu.VMEM((2, GROUPS, HALF, 8, HD), F32),
             pltpu.VMEM((GROUPS, HALF, 8, HD), F32),
             pltpu.VMEM((4, 2, HALF, 8, HD), F32),
             pltpu.VMEM((4, HALF, 8, HD), F32),
@@ -458,8 +462,8 @@
             pltpu.VMEM(v_cache.shape, BF16),
         ),
         in_specs=[pl.BlockSpec(memory_space=pltpu.SMEM)] + [vmem] * 6,
-        out_specs=(vmem, hbm, hbm, vmem, vmem),
-        scratch_shapes=[dma((2 * GROUPS,))],
+        out_specs=(hbm, hbm, hbm, vmem, vmem),
+        scratch_shapes=[pltpu.VMEM((ROWS, D), BF16), dma((2 * GROUPS + 1,))],
         input_output_aliases={1: 3, 2: 4},
         compiler_params=pltpu.CompilerParams(vmem_limit_bytes=16 * 2**20),
         name="write",

time: 49.7 us -> 47.2 us (0.950)
  Pallas kernels: 48.8 us -> 46.3 us
    pallas_call x1, Pallas kernels: 41.5 us -> 39.7 us  [device_step(): pl.pallas_call(main_kernel, out_shape=(pltpu.VMEM((GROUPS, 2, HALF, 8, HD...]
    pallas_call x1, Pallas kernels: 7.32 us -> 6.67 us  [device_step(): pl.pallas_call(write_kernel, out_shape=(jax.ShapeDtypeStruct(hidden.shape...]
where the time goes in v4:
time: 47.2 us; the launch traced here: 47 us
  Pallas kernels  46.3 us (98%)
  between operations  0.67 us (1%)
    pallas_call x1, Pallas kernels, device_step(): pl.pallas_call(main_kernel, out_shape=(pltpu.VMEM((GROUPS, 2, HALF, 8, HD...  39.7 us
    pallas_call x1, Pallas kernels, device_step(): pl.pallas_call(write_kernel, out_shape=(jax.ShapeDtypeStruct(hidden.shape...  6.67 us

profile of v4, /device:TPU:0, one launch (start us, length us, event | category | flops | bytes accessed | tf_op | source)
XLA Modules:
  0.0 47.0 jit_solution(14116454981424250287)
XLA Ops:
  0.6 0.0 copy-start
  0.6 0.0 copy-start.1
  0.7 39.7 %layer.1 = (f32[8,2,11,8,128]{4,3,2,1,0:T(8,128)S(1)}, bf16[64,512,128]{2,1,0:T(8,128)(2,1)S(1)}, bf16[64,512,128]{2,1,0:T(8,128)(2,1)S(1)}, f32[8,8,128]{2,1,0:T(8,128)S(1)}, f32[8,8,128]{2,1,0:T(8,128)S(1)}) custom-call(s32[64]{0:T(128)} %pos.1, bf16[64,2816]{1,0:T(8,128)(2,1)} %x_ref.1, f32[2816]{0:T(1024)} %g_h.1, f32[2816]{0:T(1024)} %b_h.1, ...), custom_call_target="tpu_custom_call" | custom-call | tf_op jit(solution)/shard_map/layer/pallas_call | solution.py:407
  40.3 0.0 copy-done
  40.3 0.0 copy-done.1
  40.3 6.7 %write.1 = (bf16[64,2816]{1,0:T(8,128)(2,1)}, bf16[64,512,128]{2,1,0:T(8,128)(2,1)}, bf16[64,512,128]{2,1,0:T(8,128)(2,1)}, bf16[64,512,128]{2,1,0:T(8,128)(2,1)S(1)}, bf16[64,512,128]{2,1,0:T(8,128)(2,1)S(1)}) custom-call(s32[64]{0:T(128)S(1)} %copy-done.1, ...), custom_call_target="tpu_custom_call", output_to_operand_aliasing={{3}: (1, {}), {4}: (2, {})} | custom-call | tf_op jit(solution)/shard_map/write/pallas_call | solution.py:455
Async XLA Ops:
  0.6 39.7 %copy-start = (bf16[64,2816]{1,0:T(8,128)(2,1)S(1)}, bf16[64,2816]{1,0:T(8,128)(2,1)}, u32[]{:S(2)}) copy-start(bf16[64,2816]{1,0:T(8,128)(2,1)} %x_ref.1) | copy-start | bytes 1081348
  0.6 39.7 %copy-start.1 = (s32[64]{0:T(128)S(1)}, s32[64]{0:T(128)}, u32[]{:S(2)}) copy-start(s32[64]{0:T(128)} %pos.1) | copy-start | bytes 772

commit v5 on v4

--- a/solution.py
+++ b/solution.py
@@ -61,6 +61,17 @@
     def zpeer(d):
         return (dp, ((z + d) % 4) * 4 + y * 2 + core)
 
+    sign = 1 - 2 * (z // 2)
+
+    def target(j):
+        return (z + 4 + sign * (j + 1)) % 4
+
+    def target_dev(j):
+        return (dp, target(j) * 4 + y * 2 + core)
+
+    def slot(j):
+        return 1 + sign * (1 - j)
+
     c_in = [pltpu.make_async_copy(src, dst, isem.at[i])
             for i, (src, dst) in enumerate(((x_h, x_s), (g_h, g_s), (b_h, b_s), (freq_h, freq_s), (pos_h, pos)))]
     c_up = pltpu.make_async_copy(wup, wu, wsem.at[0])
@@ -68,7 +79,7 @@
     c_q = [pltpu.make_async_copy(wqkv.at[:, pl.ds(QCHUNK * i, QCHUNK)], wq.at[i % QSLOTS], qsem.at[i]) for i in range(NQ)]
 
     def group(s):
-        return ((z + s + 1) % 4) * 2 + (y + s // 4 + 1) % 2
+        return target(s % 4) * 2 + (y + s // 4 + 1) % 2
 
     def c_kv(s):
         rows = pl.ds(8 * group(s), 8)
@@ -136,15 +147,14 @@
 
 
     def r_mly(j):
-        zt = (z + j + 1) % 4
-        return remote(mls.at[zt, 1 - y], mly.at[j], mly_s.at[j], mly_r.at[j], ypeer)
+        return remote(mls.at[target(j), 1 - y], mly.at[j], mly_s.at[j], mly_r.at[j], ypeer)
 
     def r_mlz(j):
-        return remote(mlz.at[j], mlr.at[j], mlz_s.at[j], mlz_r.at[j], zpeer(j + 1))
+        return remote(mlz.at[j], mlr.at[slot(j)], mlz_s.at[j], mlz_r.at[slot(j)], target_dev(j))
 
     def mlp_z(j):
         r_mly(j).wait_recv()
-        mlz[j] = mls[(z + j + 1) % 4, y] + mly[j]
+        mlz[j] = mls[target(j), y] + mly[j]
 
     for ch in range(NQ):
         c_q[ch].wait()
@@ -206,7 +216,7 @@
         return remote(cmb.at[j], yrcv.at[j], sty_s.at[j], sty_r.at[j], ypeer)
 
     def r_z(j):
-        return remote(zsnd.at[j], zrcv.at[j], stz_s.at[j], stz_r.at[j], zpeer(j + 1))
+        return remote(zsnd.at[j], zrcv.at[slot(j)], stz_s.at[j], stz_r.at[slot(j)], target_dev(j))
 
     lane8 = lax.broadcasted_iota(jnp.int32, (8, HD), 1)
 

time: 47.2 us -> 46.1 us (0.977); the launches traced: 47 us -> 45.3 us
  Pallas kernels: 46.3 us -> 44.6 us
    pallas_call x1, Pallas kernels: 39.7 us -> 37.9 us  [device_step(): pl.pallas_call(main_kernel, out_shape=(pltpu.VMEM((GROUPS, 2, HALF, 8, HD...]
where the time goes in v5:
time: 46.1 us; the launch traced here: 45.3 us
  Pallas kernels  44.6 us (97%)
  between operations  0.67 us (1%)
    pallas_call x1, Pallas kernels, device_step(): pl.pallas_call(main_kernel, out_shape=(pltpu.VMEM((GROUPS, 2, HALF, 8, HD...  37.9 us
    pallas_call x1, Pallas kernels, device_step(): pl.pallas_call(write_kernel, out_shape=(jax.ShapeDtypeStruct(hidden.shape...  6.67 us

profile of v5, /device:TPU:0, one launch (start us, length us, event | category | flops | bytes accessed | tf_op | source)
XLA Modules:
  0.0 45.3 jit_solution(1849492415403785237)
XLA Ops:
  0.6 0.0 copy-start
  0.6 0.0 copy-start.1
  0.7 37.9 %layer.1 = (f32[8,2,11,8,128]{4,3,2,1,0:T(8,128)S(1)}, bf16[64,512,128]{2,1,0:T(8,128)(2,1)S(1)}, bf16[64,512,128]{2,1,0:T(8,128)(2,1)S(1)}, f32[8,8,128]{2,1,0:T(8,128)S(1)}, f32[8,8,128]{2,1,0:T(8,128)S(1)}) custom-call(s32[64]{0:T(128)} %pos.1, bf16[64,2816]{1,0:T(8,128)(2,1)} %x_ref.1, f32[2816]{0:T(1024)} %g_h.1, f32[2816]{0:T(1024)} %b_h.1, ...), custom_call_target="tpu_custom_call" | custom-call | tf_op jit(solution)/shard_map/layer/pallas_call | solution.py:417
  38.6 0.0 copy-done
  38.6 0.0 copy-done.1
  38.6 6.7 %write.1 = (bf16[64,2816]{1,0:T(8,128)(2,1)}, bf16[64,512,128]{2,1,0:T(8,128)(2,1)}, bf16[64,512,128]{2,1,0:T(8,128)(2,1)}, bf16[64,512,128]{2,1,0:T(8,128)(2,1)S(1)}, bf16[64,512,128]{2,1,0:T(8,128)(2,1)S(1)}) custom-call(s32[64]{0:T(128)S(1)} %copy-done.1, ...), custom_call_target="tpu_custom_call", output_to_operand_aliasing={{3}: (1, {}), {4}: (2, {})} | custom-call | tf_op jit(solution)/shard_map/write/pallas_call | solution.py:465
Async XLA Ops:
  0.6 37.9 %copy-start = (bf16[64,2816]{1,0:T(8,128)(2,1)S(1)}, bf16[64,2816]{1,0:T(8,128)(2,1)}, u32[]{:S(2)}) copy-start(bf16[64,2816]{1,0:T(8,128)(2,1)} %x_ref.1) | copy-start | bytes 1081348
  0.6 37.9 %copy-start.1 = (s32[64]{0:T(128)S(1)}, s32[64]{0:T(128)}, u32[]{:S(2)}) copy-start(s32[64]{0:T(128)} %pos.1) | copy-start | bytes 772

commit v6 on v5

--- a/solution.py
+++ b/solution.py
@@ -24,8 +24,8 @@
 GROUPS = 8
 LANE_L = 64
 QCHUNK = 512
-NQ = 6
-QSLOTS = 4
+NQ = 3
+QHEADS = QCHUNK // HD
 F32 = jnp.float32
 BF16 = jnp.bfloat16
 
@@ -48,7 +48,7 @@
                 st, d2d, cmb, yrcv, zsnd, zrcv, ml, mld, mls, mly, mlz, mlr, wsend, wrecv,
                 isem, wsem, qsem, osem, ksem, vsem,
                 d2d_s, d2d_r, sty_s, sty_r, stz_s, stz_r, mld_s, mld_r, mly_s, mly_r, mlz_s, mlz_r, wo_s, wo_r,
-                agz_s, agz_r, agy_s, agy_r, agc_s, agc_r):
+                agz_s, agz_r, agy_s, agy_r, agc_s, agc_r, rq_s, rq_r):
     dp = lax.axis_index("dp")
     me = lax.axis_index("sp")
     core = me % 2
@@ -76,7 +76,7 @@
             for i, (src, dst) in enumerate(((x_h, x_s), (g_h, g_s), (b_h, b_s), (freq_h, freq_s), (pos_h, pos)))]
     c_up = pltpu.make_async_copy(wup, wu, wsem.at[0])
     c_dn = pltpu.make_async_copy(wdn, wd, wsem.at[1])
-    c_q = [pltpu.make_async_copy(wqkv.at[:, pl.ds(QCHUNK * i, QCHUNK)], wq.at[i % QSLOTS], qsem.at[i]) for i in range(NQ)]
+    c_q = [pltpu.make_async_copy(wqkv.at[:, pl.ds(QCHUNK * (NQ * core + i), QCHUNK)], wq.at[i], qsem.at[i]) for i in range(NQ)]
 
     def group(s):
         return target(s % 4) * 2 + (y + s // 4 + 1) % 2
@@ -94,8 +94,8 @@
 
     for c in c_in + [c_up, c_dn]:
         c.start()
-    for i in range(3):
-        c_q[i].start()
+    for c in c_q:
+        c.start()
 
     barrier = pltpu.get_barrier_semaphore()
     pl.semaphore_signal(barrier, inc=1, device_id=partner, device_id_type=MESH)
@@ -128,7 +128,6 @@
     sin = jnp.where(lax.broadcasted_iota(jnp.int32, (ROWS, HD), 1) < HD // 2, -sin, sin)
 
     c_up.wait()
-    c_q[3].start()
     up = lax.dot_general(h_s[...], wu[...], (((1,), (1,)), ((), ())), preferred_element_type=F32)
     act[...] = (0.5 * up * (1.0 + lax.erf(up * (1.0 / math.sqrt(2.0))))).astype(BF16)
     c_dn.wait()
@@ -156,30 +155,31 @@
         r_mly(j).wait_recv()
         mlz[j] = mls[target(j), y] + mly[j]
 
-    for ch in range(NQ):
-        c_q[ch].wait()
-        acc = jnp.dot(h_s[...], wq[ch % QSLOTS], preferred_element_type=F32).astype(BF16).astype(F32)
-        if ch + QSLOTS < NQ:
-            c_q[ch + QSLOTS].start()
-        if ch >= 2:
-            start_kv(ch - 2)
-        for i in range(QCHUNK // HD):
-            h = ch * (QCHUNK // HD) + i
-            vec = acc[:, HD * i:HD * (i + 1)]
-            if h <= NH:
-                vec = rope(vec, cos, sin)
-            vec = vec.reshape(GROUPS, 8, HD)
-            if h < NH:
-                q4[:, h] = vec
-            elif h == NH:
-                kn[...] = vec
-            else:
-                vn[...] = vec
-        if ch == 1:
+    def r_q(i):
+        own = q4.at[:, pl.ds(QHEADS * (NQ * core + i), QHEADS)]
+        return remote(own, own, rq_s.at[i], rq_r.at[i], partner)
+
+    start_kv(0)
+    for i in range(NQ):
+        c_q[i].wait()
+        acc = jnp.dot(h_s[...], wq[i], preferred_element_type=F32).astype(BF16).astype(F32)
+        start_kv(i + 1)
+        for t in range(QHEADS):
+            vec = acc[:, HD * t:HD * (t + 1)]
+            turned = rope(vec, cos, sin)
+            if i == NQ - 1 and t == QHEADS - 1:
+                turned = jnp.where(core == 1, vec, turned)
+            q4[:, QHEADS * (NQ * core + i) + t] = turned.reshape(GROUPS, 8, HD)
+        r_q(i).start()
+        if i == 1:
             r_mld.wait_recv()
             mls[...] = ml[1].reshape(4, 2, HALF, 8, HD) + mld[...].reshape(4, 2, HALF, 8, HD)
             for j in range(4):
                 r_mly(j).start()
+    for i in range(NQ):
+        r_q(i).wait_recv()
+    kn[...] = q4[:, NH]
+    vn[...] = q4[:, NH + 1]
 
     col_id = lax.broadcasted_iota(jnp.int32, (NH, SEQ), 1)
     sub = lax.broadcasted_iota(jnp.int32, (NH, HD), 0)
@@ -189,7 +189,7 @@
         p = group(s)
         local = [pos[8 * p + r] - me * SEQ for r in range(8)]
         inside = [(x >= 0) & (x < SEQ) for x in local]
-        qs = [q4[p, :, r, :] for r in range(8)]
+        qs = [q4[p, 0:NH, r, :] for r in range(8)]
         scores = [lax.dot_general(qs[r].astype(BF16), ko[8 * p + r], (((1,), (1,)), ((), ())), preferred_element_type=F32)
                   for r in range(8)]
         s_new = [jnp.sum(qs[r] * kn[p, r:r + 1, :], axis=-1, keepdims=True) * HD ** -0.5 for r in range(8)]
@@ -349,6 +349,8 @@
             send_c(d, o).wait_recv()
 
     r_mld.wait_send()
+    for i in range(NQ):
+        r_q(i).wait_send()
     for s in range(GROUPS):
         r_d2d(s).wait_send()
     for j in range(4):
@@ -432,12 +434,12 @@
             pltpu.VMEM((D,), F32),
             pltpu.VMEM((1, HD), F32),
             pltpu.VMEM((ROWS, HD), jnp.int32),
-            pltpu.VMEM((QSLOTS, D, QCHUNK), BF16),
+            pltpu.VMEM((NQ, D, QCHUNK), BF16),
             pltpu.VMEM((FF, D), BF16),
             pltpu.VMEM((FF, D), BF16),
             pltpu.VMEM((ROWS, D), BF16),
             pltpu.VMEM((ROWS, FF), BF16),
-            pltpu.VMEM((GROUPS, NH, 8, HD), F32),
+            pltpu.VMEM((GROUPS, NH + 2, 8, HD), F32),
             pltpu.VMEM((GROUPS, 2, HALF + 1, 8, HD), F32),
             pltpu.VMEM((GROUPS, HALF + 1, 8, HD), F32),
             pltpu.VMEM((GROUPS, HALF + 1, 8, HD), F32),
@@ -455,7 +457,7 @@
             dma((5,)), dma((2,)), dma((NQ,)), dma((2,)), dma((GROUPS,)), dma((GROUPS,)),
             dma((GROUPS,)), dma((GROUPS,)), dma((4,)), dma((4,)), dma((3,)), dma((3,)),
             dma, dma, dma((4,)), dma((4,)), dma((3,)), dma((3,)), dma, dma,
-            dma((3,)), dma((3,)), dma((4,)), dma((4,)), dma((8,)), dma((8,)),
+            dma((3,)), dma((3,)), dma((4,)), dma((4,)), dma((8,)), dma((8,)), dma((NQ,)), dma((NQ,)),
         ],
         compiler_params=pltpu.CompilerParams(collective_id=0, has_side_effects=True, vmem_limit_bytes=32 * 2**20),
         name="layer",

time: 46.1 us -> 45.2 us (0.980)
  the two profiles are of different devices: /device:TPU:0 before, /device:TPU:11 now
where the time goes in v6:
time: 45.2 us; the launch traced here: 45.1 us
  Pallas kernels  44.4 us (98%)
  between operations  0.67 us (1%)
    pallas_call x1, Pallas kernels, device_step(): pl.pallas_call(main_kernel, out_shape=(pltpu.VMEM((GROUPS, 2, HALF, 8, HD...  37.7 us
    pallas_call x1, Pallas kernels, device_step(): pl.pallas_call(write_kernel, out_shape=(jax.ShapeDtypeStruct(hidden.shape...  6.67 us

profile of v6, /device:TPU:11, one launch (start us, length us, event | category | flops | bytes accessed | tf_op | source)
XLA Modules:
  0.0 45.1 jit_solution(3446251548225274224)
XLA Ops:
  0.6 0.0 copy-start
  0.6 0.0 copy-start.1
  0.7 37.7 %layer.1 = (f32[8,2,11,8,128]{4,3,2,1,0:T(8,128)S(1)}, bf16[64,512,128]{2,1,0:T(8,128)(2,1)S(1)}, bf16[64,512,128]{2,1,0:T(8,128)(2,1)S(1)}, f32[8,8,128]{2,1,0:T(8,128)S(1)}, f32[8,8,128]{2,1,0:T(8,128)S(1)}) custom-call(s32[64]{0:T(128)} %pos.1, bf16[64,2816]{1,0:T(8,128)(2,1)} %x_ref.1, f32[2816]{0:T(1024)} %g_h.1, f32[2816]{0:T(1024)} %b_h.1, ...), custom_call_target="tpu_custom_call" | custom-call | tf_op jit(solution)/shard_map/layer/pallas_call | solution.py:419
  38.4 0.0 copy-done
  38.4 0.0 copy-done.1
  38.4 6.7 %write.1 = (bf16[64,2816]{1,0:T(8,128)(2,1)}, bf16[64,512,128]{2,1,0:T(8,128)(2,1)}, bf16[64,512,128]{2,1,0:T(8,128)(2,1)}, bf16[64,512,128]{2,1,0:T(8,128)(2,1)S(1)}, bf16[64,512,128]{2,1,0:T(8,128)(2,1)S(1)}) custom-call(s32[64]{0:T(128)S(1)} %copy-done.1, ...), custom_call_target="tpu_custom_call", output_to_operand_aliasing={{3}: (1, {}), {4}: (2, {})} | custom-call | tf_op jit(solution)/shard_map/write/pallas_call | solution.py:467
Async XLA Ops:
  0.6 37.7 %copy-start = (bf16[64,2816]{1,0:T(8,128)(2,1)S(1)}, bf16[64,2816]{1,0:T(8,128)(2,1)}, u32[]{:S(2)}) copy-start(bf16[64,2816]{1,0:T(8,128)(2,1)} %x_ref.1) | copy-start | bytes 1081348
  0.6 37.7 %copy-start.1 = (s32[64]{0:T(128)S(1)}, s32[64]{0:T(128)}, u32[]{:S(2)}) copy-start(s32[64]{0:T(128)} %pos.1) | copy-start | bytes 772

commit v7 on v6

--- a/solution.py
+++ b/solution.py
@@ -384,18 +384,20 @@
                 kw[b, tile, :] = jnp.where(here, kn[i, r:r + 1, :], ko[b, tile, :].astype(F32)).astype(BF16)
                 vw[b, tile, :] = jnp.where(here, vn[i, r:r + 1, :], vo[b, tile, :].astype(F32)).astype(BF16)
 
-        rows = pl.ds(8 * i, 8)
-        copies.append(pltpu.make_async_copy(kw.at[rows], k_out.at[rows], sem.at[2 * i]))
-        copies.append(pltpu.make_async_copy(vw.at[rows], v_out.at[rows], sem.at[2 * i + 1]))
-        copies[-2].start()
-        copies[-1].start()
+            if r % 4 == 3:
+                part = 2 * i + r // 4
+                rows = pl.ds(4 * part, 4)
+                copies.append(pltpu.make_async_copy(kw.at[rows], k_out.at[rows], sem.at[2 * part]))
+                copies.append(pltpu.make_async_copy(vw.at[rows], v_out.at[rows], sem.at[2 * part + 1]))
+                copies[-2].start()
+                copies[-1].start()
     for q in range(GROUPS // 2):
         rows = slice(16 * q, 16 * (q + 1))
         for j in range(NH):
             cols = slice(HD * j, HD * (j + 1))
             both = agb[2 * q:2 * q + 2, j // HALF, j % HALF].reshape(16, HD)
             out_ref[rows, cols] = (x_ref[rows, cols].astype(F32) + both).astype(BF16)
-    copies.append(pltpu.make_async_copy(out_ref, out, sem.at[2 * GROUPS]))
+    copies.append(pltpu.make_async_copy(out_ref, out, sem.at[4 * GROUPS]))
     copies[-1].start()
     for c in copies:
         c.wait()
@@ -475,7 +477,7 @@
         ),
         in_specs=[pl.BlockSpec(memory_space=pltpu.SMEM)] + [vmem] * 6,
         out_specs=(hbm, hbm, hbm, vmem, vmem),
-        scratch_shapes=[pltpu.VMEM((ROWS, D), BF16), dma((2 * GROUPS + 1,))],
+        scratch_shapes=[pltpu.VMEM((ROWS, D), BF16), dma((4 * GROUPS + 1,))],
         input_output_aliases={1: 3, 2: 4},
         compiler_params=pltpu.CompilerParams(vmem_limit_bytes=16 * 2**20),
         name="write",

time: 45.2 us -> 45.3 us (level)
  no operation moved by 1% of the time
where the time goes in v7:
time: 45.3 us; the launch traced here: 45.2 us
  Pallas kernels  44.5 us (98%)
  between operations  0.67 us (1%)
    pallas_call x1, Pallas kernels, device_step(): pl.pallas_call(main_kernel, out_shape=(pltpu.VMEM((GROUPS, 2, HALF, 8, HD...  37.7 us
    pallas_call x1, Pallas kernels, device_step(): pl.pallas_call(write_kernel, out_shape=(jax.ShapeDtypeStruct(hidden.shape...  6.77 us

profile of v7, /device:TPU:11, one launch (start us, length us, event | category | flops | bytes accessed | tf_op | source)
XLA Modules:
  0.0 45.2 jit_solution(5887631983229826755)
XLA Ops:
  0.6 0.0 copy-start
  0.6 0.0 copy-start.1
  0.7 37.7 %layer.1 = (f32[8,2,11,8,128]{4,3,2,1,0:T(8,128)S(1)}, bf16[64,512,128]{2,1,0:T(8,128)(2,1)S(1)}, bf16[64,512,128]{2,1,0:T(8,128)(2,1)S(1)}, f32[8,8,128]{2,1,0:T(8,128)S(1)}, f32[8,8,128]{2,1,0:T(8,128)S(1)}) custom-call(s32[64]{0:T(128)} %pos.1, bf16[64,2816]{1,0:T(8,128)(2,1)} %x_ref.1, f32[2816]{0:T(1024)} %g_h.1, f32[2816]{0:T(1024)} %b_h.1, ...), custom_call_target="tpu_custom_call" | custom-call | tf_op jit(solution)/shard_map/layer/pallas_call | solution.py:421
  38.4 0.0 copy-done
  38.4 0.0 copy-done.1
  38.4 6.8 %write.1 = (bf16[64,2816]{1,0:T(8,128)(2,1)}, bf16[64,512,128]{2,1,0:T(8,128)(2,1)}, bf16[64,512,128]{2,1,0:T(8,128)(2,1)}, bf16[64,512,128]{2,1,0:T(8,128)(2,1)S(1)}, bf16[64,512,128]{2,1,0:T(8,128)(2,1)S(1)}) custom-call(s32[64]{0:T(128)S(1)} %copy-done.1, ...), custom_call_target="tpu_custom_call", output_to_operand_aliasing={{3}: (1, {}), {4}: (2, {})} | custom-call | tf_op jit(solution)/shard_map/write/pallas_call | solution.py:469
Async XLA Ops:
  0.6 37.7 %copy-start = (bf16[64,2816]{1,0:T(8,128)(2,1)S(1)}, bf16[64,2816]{1,0:T(8,128)(2,1)}, u32[]{:S(2)}) copy-start(bf16[64,2816]{1,0:T(8,128)(2,1)} %x_ref.1) | copy-start | bytes 1081348
  0.6 37.7 %copy-start.1 = (s32[64]{0:T(128)S(1)}, s32[64]{0:T(128)}, u32[]{:S(2)}) copy-start(s32[64]{0:T(128)} %pos.1) | copy-start | bytes 772
